TPU v7x, 8 devices: a whole 2x2x1 slice. The times are simulated.
8 devices in a mesh: dp: 2 (over z, y), fsdp: 4 (over x, core).
Axes of the slice: x: 2, y: 2, z: 1, core: 2. Of those that a mesh axis runs over, the one named last changes fastest.
Arguments:
- tokens: bfloat16 [512, 77, 1024], P(('dp', 'fsdp'))
- grad_out: bfloat16 [512, 77, 1024], P(('dp', 'fsdp'))
- ln1_gain: float32 [2, 1024], P(None, 'fsdp')
- ln1_shift: float32 [2, 1024], P(None, 'fsdp')
- qkv_weight: float32 [2, 1024, 3072], P(None, 'fsdp')
- qkv_bias: float32 [2, 3072], P(None, 'fsdp')
- out_weight: float32 [2, 1024, 1024], P(None, 'fsdp')
- out_bias: float32 [2, 1024], P(None, 'fsdp')
- ln2_gain: float32 [2, 1024], P(None, 'fsdp')
- ln2_shift: float32 [2, 1024], P(None, 'fsdp')
- fc_weight: float32 [2, 1024, 4096], P(None, 'fsdp')
- fc_bias: float32 [2, 4096], P(None, 'fsdp')
- proj_weight: float32 [2, 4096, 1024], P(None, 'fsdp')
- proj_bias: float32 [2, 1024], P(None, 'fsdp')
Outputs:
- output 1: bfloat16 [512, 77, 1024], P(('dp', 'fsdp'))
- output 2: float32 [2, 1024], P(None, 'fsdp')
- output 3: float32 [2, 1024], P(None, 'fsdp')
- output 4: float32 [2, 1024, 3072], P(None, 'fsdp')
- output 5: float32 [2, 3072], P(None, 'fsdp')
- output 6: float32 [2, 1024, 1024], P(None, 'fsdp')
- output 7: float32 [2, 1024], P(None, 'fsdp')
- output 8: float32 [2, 1024], P(None, 'fsdp')
- output 9: float32 [2, 1024], P(None, 'fsdp')
- output 10: float32 [2, 1024, 4096], P(None, 'fsdp')
- output 11: float32 [2, 4096], P(None, 'fsdp')
- output 12: float32 [2, 4096, 1024], P(None, 'fsdp')
- output 13: float32 [2, 1024], P(None, 'fsdp')
All inputs are finite; a program needn't handle non-finite values.
Results may differ from a plain program's by a relative error of at most 0.0168481.
Values are sent between devices in bfloat16 or wider.
A program may use at most 1 GiB of HBM per device.

v0:
```python
import jax
import jax.numpy as jnp
from jax import lax
from jax.sharding import PartitionSpec as P

HEAD_DIM = 64
NORM_EPS = 1e-5
RANKS = (2, 2, 3, 2, 3, 2, 2, 2, 3, 2, 3, 2)


def norm_fwd(source, gain, shift):
    src32 = source.astype(jnp.float32)
    centered = src32 - jnp.mean(src32, axis=-1, keepdims=True)
    inv_std = lax.rsqrt(jnp.mean(centered * centered, axis=-1, keepdims=True) + NORM_EPS)
    return (centered * inv_std * gain.astype(jnp.float32) + shift.astype(jnp.float32)).astype(jnp.bfloat16)


def norm_bwd(d_out, source, gain, want_input):
    src32 = source.astype(jnp.float32)
    centered = src32 - jnp.mean(src32, axis=-1, keepdims=True)
    inv_std = lax.rsqrt(jnp.mean(centered * centered, axis=-1, keepdims=True) + NORM_EPS)
    normed = centered * inv_std
    d_gain = jnp.sum(d_out * normed, axis=(0, 1))
    d_shift = jnp.sum(d_out, axis=(0, 1))
    if not want_input:
        return None, d_gain, d_shift
    d_norm = d_out * gain.astype(jnp.float32)
    d_source = inv_std * (d_norm - jnp.mean(d_norm, axis=-1, keepdims=True) - normed * jnp.mean(d_norm * normed, axis=-1, keepdims=True))
    return d_source, d_gain, d_shift


def gelu_grad(pre_act):
    cdf = 0.5 * (1.0 + lax.erf(pre_act * 0.7071067811865476))
    return cdf + pre_act * jnp.exp(-0.5 * pre_act * pre_act) * 0.3989422804014327


def split_qkv(qkv, heads):
    grouped = qkv.reshape(qkv.shape[0], qkv.shape[1], 3, heads, HEAD_DIM)
    return grouped[:, :, 0], grouped[:, :, 1], grouped[:, :, 2]


def attn_fwd(qkv, heads):
    query, keys, values = split_qkv(qkv, heads)
    length = qkv.shape[1]
    scores = jnp.einsum('bqhd,bkhd->bhqk', query, keys, preferred_element_type=jnp.float32) * (HEAD_DIM ** -0.5)
    causal = lax.broadcasted_iota(jnp.int32, (length, length), 0) >= lax.broadcasted_iota(jnp.int32, (length, length), 1)
    probs = jax.nn.softmax(jnp.where(causal, scores, -1e30), axis=-1)
    context = jnp.einsum('bhqk,bkhd->bqhd', probs.astype(jnp.bfloat16), values, preferred_element_type=jnp.float32)
    return context.astype(jnp.bfloat16).reshape(qkv.shape[0], length, heads * HEAD_DIM), probs


def attn_bwd(d_context, qkv, probs, heads):
    query, keys, values = split_qkv(qkv, heads)
    d_heads = d_context.reshape(query.shape)
    d_values = jnp.einsum('bhqk,bqhd->bkhd', probs.astype(jnp.bfloat16), d_heads, preferred_element_type=jnp.float32)
    d_probs = jnp.einsum('bqhd,bkhd->bhqk', d_heads, values, preferred_element_type=jnp.float32).astype(jnp.bfloat16).astype(jnp.float32)
    d_scores = probs * (d_probs - jnp.sum(d_probs * probs, axis=-1, keepdims=True)) * (HEAD_DIM ** -0.5)
    d_scores = d_scores.astype(jnp.bfloat16)
    d_query = jnp.einsum('bhqk,bkhd->bqhd', d_scores, keys, preferred_element_type=jnp.float32)
    d_keys = jnp.einsum('bhqk,bqhd->bkhd', d_scores, query, preferred_element_type=jnp.float32)
    d_qkv = jnp.stack([d_query.astype(jnp.bfloat16), d_keys.astype(jnp.bfloat16), d_values.astype(jnp.bfloat16)], axis=2)
    return d_qkv.reshape(qkv.shape)


def block_fwd(tokens, layer):
    ln1_gain, ln1_shift, qkv_weight, qkv_bias, out_weight, out_bias, ln2_gain, ln2_shift, fc_weight, fc_bias, proj_weight, proj_bias = layer
    heads = qkv_weight.shape[0] // HEAD_DIM
    normed1 = norm_fwd(tokens, ln1_gain, ln1_shift)
    qkv = (jnp.einsum('btw,wc->btc', normed1, qkv_weight, preferred_element_type=jnp.float32) + qkv_bias.astype(jnp.float32)).astype(jnp.bfloat16)
    context, probs = attn_fwd(qkv, heads)
    middle = (tokens.astype(jnp.float32) + jnp.einsum('btw,wv->btv', context, out_weight, preferred_element_type=jnp.float32) + out_bias.astype(jnp.float32)).astype(jnp.bfloat16)
    normed2 = norm_fwd(middle, ln2_gain, ln2_shift)
    pre_act = jnp.einsum('btw,wf->btf', normed2, fc_weight, preferred_element_type=jnp.float32) + fc_bias.astype(jnp.float32)
    hidden = jax.nn.gelu(pre_act, approximate=False).astype(jnp.bfloat16)
    result = (middle.astype(jnp.float32) + jnp.einsum('btf,fw->btw', hidden, proj_weight, preferred_element_type=jnp.float32) + proj_bias.astype(jnp.float32)).astype(jnp.bfloat16)
    return result, (tokens, normed1, qkv, probs, context, middle, normed2, pre_act, hidden)


def block_bwd(d_result, saved, layer, want_input):
    ln1_gain, _, qkv_weight, _, out_weight, _, ln2_gain, _, fc_weight, _, proj_weight, _ = layer
    tokens, normed1, qkv, probs, context, middle, normed2, pre_act, hidden = saved
    heads = qkv_weight.shape[0] // HEAD_DIM
    d_res32 = d_result.astype(jnp.float32)
    g_proj_bias = jnp.sum(d_res32, axis=(0, 1))
    g_proj_weight = jnp.einsum('btf,btw->fw', hidden, d_result, preferred_element_type=jnp.float32)
    d_hidden = jnp.einsum('btw,fw->btf', d_result, proj_weight, preferred_element_type=jnp.float32).astype(jnp.bfloat16).astype(jnp.float32)
    d_pre = d_hidden * gelu_grad(pre_act)
    g_fc_bias = jnp.sum(d_pre, axis=(0, 1))
    d_pre = d_pre.astype(jnp.bfloat16)
    g_fc_weight = jnp.einsum('btw,btf->wf', normed2, d_pre, preferred_element_type=jnp.float32)
    d_normed2 = jnp.einsum('btf,wf->btw', d_pre, fc_weight, preferred_element_type=jnp.float32).astype(jnp.bfloat16).astype(jnp.float32)
    d_mid_norm, g_ln2_gain, g_ln2_shift = norm_bwd(d_normed2, middle, ln2_gain, True)
    d_middle = (d_res32 + d_mid_norm).astype(jnp.bfloat16)
    g_out_bias = jnp.sum(d_middle, axis=(0, 1), dtype=jnp.float32)
    g_out_weight = jnp.einsum('btw,btv->wv', context, d_middle, preferred_element_type=jnp.float32)
    d_context = jnp.einsum('btv,wv->btw', d_middle, out_weight, preferred_element_type=jnp.float32).astype(jnp.bfloat16)
    d_qkv = attn_bwd(d_context, qkv, probs, heads)
    g_qkv_bias = jnp.sum(d_qkv, axis=(0, 1), dtype=jnp.float32)
    g_qkv_weight = jnp.einsum('btw,btc->wc', normed1, d_qkv, preferred_element_type=jnp.float32)
    d_normed1 = jnp.einsum('btc,wc->btw', d_qkv, qkv_weight, preferred_element_type=jnp.float32).astype(jnp.bfloat16).astype(jnp.float32)
    d_tok_norm, g_ln1_gain, g_ln1_shift = norm_bwd(d_normed1, tokens, ln1_gain, want_input)
    d_tokens = None
    if want_input:
        d_tokens = (d_middle.astype(jnp.float32) + d_tok_norm).astype(jnp.bfloat16)
    grads = (g_ln1_gain, g_ln1_shift, g_qkv_weight, g_qkv_bias, g_out_weight, g_out_bias, g_ln2_gain, g_ln2_shift, g_fc_weight, g_fc_bias, g_proj_weight, g_proj_bias)
    return d_tokens, grads


def solution(mesh):
    batch_spec = P(('dp', 'fsdp'), None, None)
    param_specs = tuple(P(None, 'fsdp', None) if rank == 3 else P(None, 'fsdp') for rank in RANKS)

    def gather_layer(shards, index):
        return tuple(lax.all_gather(shard[index].astype(jnp.bfloat16), 'fsdp', axis=0, tiled=True) for shard in shards)

    def reduce_grads(grads):
        return tuple(lax.psum(lax.psum_scatter(grad, 'fsdp', scatter_dimension=0, tiled=True), 'dp') for grad in grads)

    def per_device(tokens, grad_out, *shards):
        mid_tokens, saved0 = block_fwd(tokens, gather_layer(shards, 0))
        block_out, saved1 = block_fwd(mid_tokens, gather_layer(shards, 1))
        d_mid, grads1 = block_bwd(grad_out, saved1, gather_layer(shards, 1), True)
        sums1 = reduce_grads(grads1)
        _, grads0 = block_bwd(d_mid, saved0, gather_layer(shards, 0), False)
        sums0 = reduce_grads(grads0)
        return (block_out,) + tuple(jnp.stack([grad_a, grad_b]) for grad_a, grad_b in zip(sums0, sums1))

    return jax.shard_map(per_device, mesh=mesh, in_specs=(batch_spec, batch_spec) + param_specs, out_specs=(batch_spec,) + param_specs, check_vma=False)
```

profile of v0, /device:TPU:0, one launch (start us, length us, event | category | flops | bytes accessed | tf_op | source)
XLA Modules:
  0.0 3973.8 jit_solution(12509355375948197444)
XLA Ops:
  180.9 50.5 %add_convert_fusion.1 = bf16[64,77,3072]{2,1,0:T(8,128)(2,1)} fusion(f32[3072]{0:T(1024)S(1)} %bitcast.281, bf16[1,1024,3072]{2,1,0:T(8,128)(2,1)} %all-gather.33.cloned.1.call-done, f32[1024]{0:T(1024)S(1)} %bitcast.284, f32[1024]{0:T(1024)S(1)} %bitcast.282, f32[64,77]{1,0:T(8,128)S(1)} %add_rsqrt_fusion.3, f32[64,77]{1,0:T(8,128)S(1)} %broadcast_multiply_fusion.9, ...), kind=kOutput, calls=%fused_computation.57 | convolution fusion | flops 31064850432 | bytes 46721536 | tf_op jit(solution)/shard_map/btw,wc->btc/dot_general | solution.py:69
  231.5 66.8 %reshape.252 = bf16[64,77,3,16,64]{4,3,2,1,0:T(8,128)(2,1)} reshape(bf16[64,77,3072]{2,1,0:T(8,128)(2,1)} %add_convert_fusion.1) | data formatting | bytes 60555264 | tf_op jit(solution)/shard_map/reshape | solution.py:38
  298.2 39.3 fusion.234
  413.5 26.5 fusion.132
  440.0 47.5 %fusion.247 = (f32[64,16,77]{2,1,0:T(8,128)S(1)}, f32[64,16,77,77]{2,3,1,0:T(8,128)}) fusion(f32[64,16,77,77]{2,3,1,0:T(8,128)} %fusion.132, pred[77,77]{0,1:T(8,128)(4,1)S(1)} %copy-done.49), kind=kOutput, calls=%fused_computation.309 | output fusion | flops 36427852 | bytes 48891688 | tf_op jit(solution)/shard_map/sub | solution.py:47
  487.5 26.0 fusion.164
  513.5 34.1 convert_reduce_fusion.7
  567.0 224.6 %fusion.6 = (bf16[64,77,4096]{2,1,0:T(8,128)(2,1)}, f32[64,77,4096]{2,1,0:T(8,128)}) fusion(f32[4096]{0:T(1024)S(1)} %bitcast.274, bf16[1,1024,4096]{2,1,0:T(8,128)(2,1)} %all-gather.37.cloned.1.call-done, bf16[64,77,1024]{2,1,0:T(8,128)(2,1)} %fusion.207.clone.4), kind=kOutput, calls=%fused_computation.12 | convolution fusion | flops 42671276032 | bytes 139608064 | tf_op jit(solution)/shard_map/btw,wf->btf/dot_general | solution.py:73
  791.7 52.3 %convert_reduce_fusion.6 = (f32[64,77]{1,0:T(8,128)S(1)}, bf16[64,77,1024]{2,1,0:T(8,128)(2,1)}) fusion(f32[1024]{0:T(1024)S(1)} %bitcast.290, bf16[64,77,4096]{2,1,0:T(8,128)(2,1)} %get-tuple-element.151, bf16[1,4096,1024]{2,1,0:T(8,128)(2,1)} %all-gather.39.cloned.1.call-done, bf16[64,77,1024]{2,1,0:T(8,128)(2,1)} %get-tuple-element.150), kind=kOutput, calls=%fused_computation.90 | convolution fusion | flops 41369333760 | bytes 68967680 | tf_op jit(solution)/shard_map/btf,fw->btw/dot_general | solution.py:75
  851.2 41.3 %add_convert_fusion = bf16[64,77,3072]{2,1,0:T(8,128)(2,1)} fusion(f32[3072]{0:T(1024)S(1)} %bitcast.280, bf16[1,1024,3072]{2,1,0:T(8,128)(2,1)} %all-gather.41.cloned.1.call-done, bf16[64,77,1024]{2,1,0:T(8,128)(2,1)} %get-tuple-element.154, f32[1024]{0:T(1024)S(1)} %bitcast.286, f32[1024]{0:T(1024)S(1)} %bitcast.270, f32[64,77]{1,0:T(8,128)S(1)} %add_rsqrt_fusion.1, ...), kind=kOutput, calls=%fused_computation.56 | convolution fusion | flops 31064850432 | bytes 46721536 | tf_op jit(solution)/shard_map/btw,wc->btc/dot_general | solution.py:69
  892.5 66.8 %reshape.253 = bf16[64,77,3,16,64]{4,3,2,1,0:T(8,128)(2,1)} reshape(bf16[64,77,3072]{2,1,0:T(8,128)(2,1)} %add_convert_fusion) | data formatting | bytes 60555264 | tf_op jit(solution)/shard_map/reshape | solution.py:38
  959.3 39.4 fusion.233
  998.7 25.3 copy.158
  1024.0 25.3 copy.159
  1049.3 26.3 fusion.123
  1075.7 48.2 %fusion.248 = (f32[64,16,77]{2,1,0:T(8,128)S(1)}, f32[64,16,77,77]{2,3,1,0:T(8,128)}) fusion(f32[64,16,77,77]{2,3,1,0:T(8,128)} %fusion.123, pred[77,77]{0,1:T(8,128)(4,1)S(1)} %copy-done.50), kind=kOutput, calls=%fused_computation.310 | output fusion | flops 36427852 | bytes 48891688 | tf_op jit(solution)/shard_map/sub | solution.py:47
  1123.9 25.5 copy.157
  1149.4 25.8 fusion.169
  1218.0 224.5 %fusion.9 = (bf16[64,77,4096]{2,1,0:T(8,128)(2,1)}, f32[64,77,4096]{2,1,0:T(8,128)}) fusion(f32[4096]{0:T(1024)S(1)} %bitcast.276, bf16[1,1024,4096]{2,1,0:T(8,128)(2,1)} %all-gather.45.cloned.1.call-done, bf16[64,77,1024]{2,1,0:T(8,128)(2,1)} %fusion.211.clone.2), kind=kOutput, calls=%fused_computation.15 | convolution fusion | flops 42671276032 | bytes 139608064 | tf_op jit(solution)/shard_map/btw,wf->btf/dot_general | solution.py:73
  1442.5 86.4 %fusion.249 = (f32[4096]{0:T(1024)}, bf16[64,77,4096]{2,1,0:T(8,128)(2,1)}) fusion(f32[64,77,4096]{2,1,0:T(8,128)} %get-tuple-element.160, f32[4096]{0:T(1024)S(1)} %bitcast.277, bf16[1,4096,1024]{2,1,0:T(8,128)(2,1)} %all-gather.47.cloned.1.call-done, bf16[64,77,1024]{2,0,1:T(8,128)(2,1)} %param.15), kind=kOutput, calls=%fused_computation.311 | convolution fusion | flops 41621647360 | bytes 139624448 | tf_op jit(solution)/shard_map/btw,fw->btf/dot_general | solution.py:86
  1529.0 57.5 %fusion.101 = (f32[1024]{0:T(1024)}, f32[64,77]{1,0:T(8,128)S(1)}, f32[64,77]{1,0:T(8,128)S(1)}, f32[1024]{0:T(1024)}, bf16[64,77,1024]{2,1,0:T(8,128)(2,1)}) fusion(bf16[64,77,1024]{2,1,0:T(8,128)(2,1)} %get-tuple-element.158, f32[64,77]{1,0:T(8,128)S(1)} %copy-done.13, f32[64,77]{1,0:T(8,128)S(1)} %copy-done.7, f32[1024]{0:T(1024)S(1)} %bitcast.263, ...), kind=kOutput, calls=%fused_computation.164 | convolution fusion | flops 41399607296 | bytes 69035008 | tf_op jit(solution)/shard_map/btf,wf->btw/dot_general | solution.py:91
  1659.1 58.5 %convert_bitcast_fusion.5 = bf16[64,77,1,16,64]{1,4,3,0,2:T(8,128)(2,1)} fusion(bf16[64,16,77,77]{2,3,1,0:T(8,128)(2,1)} %fusion.143, bf16[64,77,1,16,64]{1,4,3,0,2:T(8,128)(2,1)} %copy.159, f32[64,16,77,77]{2,3,1,0:T(8,128)} %get-tuple-element.156, f32[64,16,77]{2,1,0:T(8,128)S(1)} %copy-done.75), kind=kOutput, calls=%fused_computation.211 | convolution fusion | flops 836892736 | bytes 56928256 | tf_op jit(solution)/shard_map/bhqk,bkhd->bqhd/dot_general | solution.py:59
  1717.7 58.9 %convert_bitcast_fusion.4 = bf16[64,77,1,16,64]{1,4,3,0,2:T(8,128)(2,1)} fusion(bf16[64,16,77,77]{2,3,1,0:T(8,128)(2,1)} %fusion.143, bf16[64,77,1,16,64]{1,4,3,0,2:T(8,128)(2,1)} %copy.158, f32[64,16,77,77]{2,3,1,0:T(8,128)} %get-tuple-element.156, f32[64,16,77]{2,1,0:T(8,128)S(1)} %copy-done.75), kind=kOutput, calls=%fused_computation.210 | convolution fusion | flops 836892736 | bytes 56928256 | tf_op jit(solution)/shard_map/bhqk,bqhd->bkhd/dot_general | solution.py:60
  1776.6 27.1 convert_bitcast_fusion.3
  1803.7 34.5 convert_reduce_fusion
  1838.1 74.2 %copy.147 = bf16[64,77,3,16,64]{4,3,2,1,0:T(8,128)(2,1)} copy(bf16[64,77,3,16,64]{1,4,3,0,2:T(8,128)(2,1)} %get-tuple-element.115) | data formatting | bytes 60555264 | tf_op jit(solution)/shard_map/reshape | solution.py:62
  1912.3 70.1 %reshape.255 = bf16[64,77,3072]{2,1,0:T(8,128)(2,1)} reshape(bf16[64,77,3,16,64]{4,3,2,1,0:T(8,128)(2,1)} %copy.147) | data formatting | bytes 60555264 | tf_op jit(solution)/shard_map/reshape | solution.py:62
  1982.4 47.3 %fusion.91 = (f32[64,77]{1,0:T(8,128)S(1)}, f32[1024]{0:T(1024)}, f32[64,77]{1,0:T(8,128)S(1)}, f32[1024]{0:T(1024)}, bf16[64,77,1024]{2,1,0:T(8,128)(2,1)}) fusion(bf16[64,77,1024]{2,1,0:T(8,128)(2,1)} %get-tuple-element.154, f32[1024]{0:T(1024)S(1)} %bitcast.271, f32[64,77]{1,0:T(8,128)S(1)} %copy-done.25, f32[64,77]{1,0:T(8,128)S(1)} %copy-done.19, ...), kind=kOutput, calls=%fused_computation.154 | convolution fusion | flops 31064842240 | bytes 56845312 | tf_op jit(solution)/shard_map/btc,wc->btw/dot_general | solution.py:100
  2049.2 79.2 %fusion.250 = (f32[4096]{0:T(1024)}, bf16[64,77,4096]{2,1,0:T(8,128)(2,1)}) fusion(f32[64,77,4096]{2,1,0:T(8,128)} %get-tuple-element.152, f32[4096]{0:T(1024)S(1)} %bitcast.275, bf16[64,77,1024]{2,1,0:T(8,128)(2,1)} %get-tuple-element.107, bf16[1,4096,1024]{2,1,0:T(8,128)(2,1)} %all-gather.39.cloned.1.call-done), kind=kOutput, calls=%fused_computation.312 | convolution fusion | flops 41621647360 | bytes 139624448 | tf_op jit(solution)/shard_map/btw,fw->btf/dot_general | solution.py:86
  2128.4 57.4 %fusion.103 = (f32[1024]{0:T(1024)}, f32[64,77]{1,0:T(8,128)S(1)}, f32[64,77]{1,0:T(8,128)S(1)}, f32[1024]{0:T(1024)}, bf16[64,77,1024]{2,1,0:T(8,128)(2,1)}) fusion(bf16[64,77,1024]{2,1,0:T(8,128)(2,1)} %get-tuple-element.150, f32[64,77]{1,0:T(8,128)S(1)} %copy-done.16, f32[64,77]{1,0:T(8,128)S(1)} %copy-done.10, f32[1024]{0:T(1024)S(1)} %bitcast.259, ...), kind=kOutput, calls=%fused_computation.166 | convolution fusion | flops 41399607296 | bytes 69035008 | tf_op jit(solution)/shard_map/btf,wf->btw/dot_general | solution.py:91
  2277.0 59.6 %convert_bitcast_fusion.2 = bf16[64,77,1,16,64]{1,4,3,0,2:T(8,128)(2,1)} fusion(bf16[64,16,77,77]{2,3,1,0:T(8,128)(2,1)} %fusion.140, bf16[64,77,1,16,64]{1,4,3,0,2:T(8,128)(2,1)} %copy.156, f32[64,16,77,77]{2,3,1,0:T(8,128)} %get-tuple-element.148, f32[64,16,77]{2,1,0:T(8,128)S(1)} %copy-done.73), kind=kOutput, calls=%fused_computation.208 | convolution fusion | flops 836892736 | bytes 56928256 | tf_op jit(solution)/shard_map/bhqk,bkhd->bqhd/dot_general | solution.py:59
  2356.0 27.1 convert_bitcast_fusion
  2383.2 59.5 %convert_bitcast_fusion.1 = bf16[64,77,1,16,64]{1,4,3,0,2:T(8,128)(2,1)} fusion(bf16[64,16,77,77]{2,3,1,0:T(8,128)(2,1)} %fusion.140, bf16[64,77,1,16,64]{1,4,3,0,2:T(8,128)(2,1)} %copy.155, f32[64,16,77,77]{2,3,1,0:T(8,128)} %get-tuple-element.148, f32[64,16,77]{2,1,0:T(8,128)S(1)} %copy-done.73), kind=kOutput, calls=%fused_computation.207 | convolution fusion | flops 836892736 | bytes 56928256 | tf_op jit(solution)/shard_map/bhqk,bqhd->bkhd/dot_general | solution.py:60
  2442.7 34.0 convert_reduce_fusion.1
  2476.7 74.5 %copy.151 = bf16[64,77,3,16,64]{4,3,2,1,0:T(8,128)(2,1)} copy(bf16[64,77,3,16,64]{1,4,3,0,2:T(8,128)(2,1)} %get-tuple-element.113) | data formatting | bytes 60555264 | tf_op jit(solution)/shard_map/reshape | solution.py:62
  2551.1 70.2 %reshape.257 = bf16[64,77,3072]{2,1,0:T(8,128)(2,1)} reshape(bf16[64,77,3,16,64]{4,3,2,1,0:T(8,128)(2,1)} %copy.151) | data formatting | bytes 60555264 | tf_op jit(solution)/shard_map/reshape | solution.py:62
  2621.4 67.4 %convolution_bitcast_fusion.3 = f32[1024,3072]{1,0:T(8,128)} fusion(bf16[64,77,3072]{2,1,0:T(8,128)(2,1)} %reshape.257, f32[1024]{0:T(1024)S(1)} %bitcast.285, f32[1024]{0:T(1024)S(1)} %bitcast.283, f32[64,77]{1,0:T(8,128)S(1)} %copy-done.36, f32[64,77]{1,0:T(8,128)S(1)} %copy-done.22, bf16[64,77,1024]{2,0,1:T(8,128)(2,1)} %param.14), kind=kOutput, calls=%fused_computation.247 | convolution fusion | flops 31034572800 | bytes 53000704 | tf_op jit(solution)/shard_map/btw,btc->wc/dot_general | solution.py:99
  2688.9 44.3 %convolution_bitcast_fusion.2 = f32[1024,3072]{1,0:T(8,128)} fusion(bf16[64,77,3072]{2,1,0:T(8,128)(2,1)} %reshape.255, bf16[64,77,1024]{2,1,0:T(8,128)(2,1)} %get-tuple-element.154, f32[1024]{0:T(1024)S(1)} %bitcast.287, f32[1024]{0:T(1024)S(1)} %bitcast.273, f32[64,77]{1,0:T(8,128)S(1)} %copy-done.26, f32[64,77]{1,0:T(8,128)S(1)} %copy-done.20), kind=kOutput, calls=%fused_computation.246 | convolution fusion | flops 31034572800 | bytes 53000704 | tf_op jit(solution)/shard_map/btw,btc->wc/dot_general | solution.py:99
  2733.4 53.6 %convolution_bitcast_fusion.1 = f32[4096,1024]{1,0:T(8,128)} fusion(bf16[64,77,4096]{2,1,0:T(8,128)(2,1)} %get-tuple-element.151, bf16[64,77,1024]{2,1,0:T(8,128)(2,1)} %get-tuple-element.107), kind=kOutput, calls=%fused_computation.225 | convolution fusion | flops 41339060224 | bytes 67239936 | tf_op jit(solution)/shard_map/btf,btw->fw/dot_general | solution.py:85
  2787.2 56.3 %fusion.177 = f32[1024,4096]{1,0:T(8,128)} fusion(bf16[64,77,4096]{2,1,0:T(8,128)(2,1)} %get-tuple-element.167, bf16[64,77,1024]{2,1,0:T(8,128)(2,1)} %get-tuple-element.150, f32[1024]{0:T(1024)S(1)} %bitcast.267, f32[1024]{0:T(1024)S(1)} %bitcast.261, f32[64,77]{1,0:T(8,128)S(1)} %copy-done.17, f32[64,77]{1,0:T(8,128)S(1)} %copy-done.11), kind=kOutput, calls=%fused_computation.223 | convolution fusion | flops 41369337856 | bytes 67287552 | tf_op jit(solution)/shard_map/btw,btf->wf/dot_general | solution.py:90
  2843.6 56.8 %fusion.174 = f32[1024,4096]{1,0:T(8,128)} fusion(bf16[64,77,4096]{2,1,0:T(8,128)(2,1)} %get-tuple-element.165, bf16[64,77,1024]{2,1,0:T(8,128)(2,1)} %get-tuple-element.158, f32[1024]{0:T(1024)S(1)} %bitcast.269, f32[1024]{0:T(1024)S(1)} %bitcast.265, f32[64,77]{1,0:T(8,128)S(1)} %copy-done.14, f32[64,77]{1,0:T(8,128)S(1)} %copy-done.8), kind=kOutput, calls=%fused_computation.222 | convolution fusion | flops 41369337856 | bytes 67287552 | tf_op jit(solution)/shard_map/btw,btf->wf/dot_general | solution.py:90
  2900.5 86.5 %convolution_bitcast_fusion = f32[4096,1024]{1,0:T(8,128)} fusion(bf16[64,77,4096]{2,1,0:T(8,128)(2,1)} %get-tuple-element.159, bf16[64,77,1024]{2,0,1:T(8,128)(2,1)} %param.15), kind=kOutput, calls=%fused_computation.224 | convolution fusion | flops 41339060224 | bytes 67239936 | tf_op jit(solution)/shard_map/btf,btw->fw/dot_general | solution.py:85
  2988.5 44.7 %convert_reduce_fusion.9 = (f32[1024]{0:T(1024)}, f32[1024]{0:T(1024)}) fusion(f32[64,77]{1,0:T(8,128)S(1)} %copy-done.37, f32[64,77]{1,0:T(8,128)S(1)} %copy-done.23, bf16[64,77,1024]{2,0,1:T(8,128)(2,1)} %param.14, bf16[64,77,3072]{2,1,0:T(8,128)(2,1)} %reshape.257, bf16[1,1024,3072]{2,1,0:T(8,128)(2,1)} %all-gather.33.cloned.1.call-done), kind=kOutput, calls=%fused_computation.108 | convolution fusion | flops 31044665344 | bytes 46709248 | tf_op jit(solution)/shard_map/btc,wc->btw/dot_general | solution.py:100
  3033.4 81.9 %reduce-scatter.17.cloned.1.call-done = f32[256,4096]{1,0:T(8,128)} async-done(((f32[1024,4096]{1,0:T(8,128)}), f32[256,4096]{1,0:T(8,128)}) %reduce-scatter.17.cloned.1.call-update) | async-done | bytes 4194320 | tf_op jit(solution)/shard_map/reduce_scatter | solution.py:117
  3115.3 121.2 %reduce-scatter.19.cloned.1.call-done = f32[256,4096]{1,0:T(8,128)} async-done(((f32[1024,4096]{1,0:T(8,128)}), f32[256,4096]{1,0:T(8,128)}) %reduce-scatter.19.cloned.1.call-update) | async-done | bytes 4194320 | tf_op jit(solution)/shard_map/reduce_scatter | solution.py:117
  3236.5 121.2 %reduce-scatter.23.cloned.1.call-done = f32[1024,1024]{1,0:T(8,128)} async-done(((f32[4096,1024]{1,0:T(8,128)}), f32[1024,1024]{1,0:T(8,128)}) %reduce-scatter.23.cloned.1.call-update) | async-done | bytes 4194320 | tf_op jit(solution)/shard_map/reduce_scatter | solution.py:117
  3367.1 51.1 %fusion.100 = bf16[64,77,1024]{2,1,0:T(8,128)(2,1)} fusion(bf16[64,77,1024]{2,1,0:T(8,128)(2,1)} %get-tuple-element.158, f32[1024]{0:T(1024)S(1)} %bitcast.291, bf16[64,77,4096]{2,1,0:T(8,128)(2,1)} %get-tuple-element.159, bf16[1,4096,1024]{2,1,0:T(8,128)(2,1)} %all-gather.47.cloned.1.call-done), kind=kOutput, calls=%fused_computation.163 | convolution fusion | flops 41359245312 | bytes 68947968 | tf_op jit(solution)/shard_map/btf,fw->btw/dot_general | solution.py:75
  3457.9 487.8 %all-reduce.24.cloned.1.call-done = (f32[1,256,3072]{2,1,0:T(8,128)}, f32[1,256,3072]{2,1,0:T(8,128)}, f32[1,256,1024]{2,1,0:T(8,128)}, f32[1,256,1024]{2,1,0:T(...) async-done(((f32[1,256,3072]{2,1,0:T(8,128)}, f32[1,256,3072]{2,1,0:T(8,128)}, ...) | async-done | bytes 25165840 | tf_op jit(solution)/shard_map/psum | solution.py:117
  (329 shorter events, 591.4 us)
Async XLA Ops:
  7.2 173.7 %all-gather.33.cloned.1.call-start = ((), (), s32[]{:S(2)}) async-start(), calls=%async_computation.16 | async-start | bytes 7864320 | tf_op jit(solution)/shard_map/all_gather | solution.py:114
  12.4 501.0 %all-gather.35.cloned.1.call-start = ((), (), s32[]{:S(2)}) async-start(), calls=%async_computation.17 | async-start | bytes 2621440 | tf_op jit(solution)/shard_map/all_gather | solution.py:114
  15.3 551.7 %all-gather.37.cloned.1.call-start = ((), (), s32[]{:S(2)}) async-start(), calls=%async_computation.18 | async-start | bytes 10485760 | tf_op jit(solution)/shard_map/all_gather | solution.py:114
  21.7 770.0 %all-gather.39.cloned.1.call-start = ((), (), s32[]{:S(2)}) async-start(), calls=%async_computation.19 | async-start | bytes 10485760 | tf_op jit(solution)/shard_map/all_gather | solution.py:114
  25.8 71.6 %copy-start.67 = (f32[2,256]{1,0:T(2,128)S(1)}, f32[2,256]{1,0:T(2,128)}, u32[]{:S(2)}) copy-start(f32[2,256]{1,0:T(2,128)} %param.23) | copy-start | bytes 6148
  25.8 79.0 %copy-start.51 = (f32[2,1024]{1,0:T(2,128)S(1)}, f32[2,1024]{1,0:T(2,128)}, u32[]{:S(2)}) copy-start(f32[2,1024]{1,0:T(2,128)} %param.25) | copy-start | bytes 24580
  25.9 88.5 %copy-start.68 = (f32[2,256]{1,0:T(2,128)S(1)}, f32[2,256]{1,0:T(2,128)}, u32[]{:S(2)}) copy-start(f32[2,256]{1,0:T(2,128)} %param.27) | copy-start | bytes 6148
  28.3 822.8 %all-gather.41.cloned.1.call-start = ((), (), s32[]{:S(2)}) async-start(), calls=%async_computation.20 | async-start | bytes 7864320 | tf_op jit(solution)/shard_map/all_gather | solution.py:114
  28.9 1146.3 %all-gather.43.cloned.1.call-start = ((), (), s32[]{:S(2)}) async-start(), calls=%async_computation.21 | async-start | bytes 2621440 | tf_op jit(solution)/shard_map/all_gather | solution.py:114
  29.5 1188.5 %all-gather.45.cloned.1.call-start = ((), (), s32[]{:S(2)}) async-start(), calls=%async_computation.22 | async-start | bytes 10485760 | tf_op jit(solution)/shard_map/all_gather | solution.py:114
  30.3 1412.2 %all-gather.47.cloned.1.call-start = ((), (), s32[]{:S(2)}) async-start(), calls=%async_computation.23 | async-start | bytes 10485760 | tf_op jit(solution)/shard_map/all_gather | solution.py:114
  31.0 3002.3 %reduce-scatter.13.cloned.1.call-start = ((), (), s32[]{:S(2)}) async-start(), calls=%async_computation.10 | async-start | bytes 5242880 | tf_op jit(solution)/shard_map/reduce_scatter | solution.py:117
  41.4 190.0 %copy-start.21 = (f32[64,77]{1,0:T(8,128)}, f32[64,77]{1,0:T(8,128)S(1)}, u32[]{:S(2)}) copy-start(f32[64,77]{1,0:T(8,128)S(1)} %broadcast_multiply_fusion.9) | copy-start | bytes 59140
  55.8 175.6 %copy-start.35 = (f32[64,77]{1,0:T(8,128)}, f32[64,77]{1,0:T(8,128)S(1)}, u32[]{:S(2)}) copy-start(f32[64,77]{1,0:T(8,128)S(1)} %add_rsqrt_fusion.3) | copy-start | bytes 59140
  65.7 165.8 %copy-start.53 = (f32[1,1024]{1,0:T(1,128)}, f32[1,1024]{1,0:T(1,128)S(1)}, u32[]{:S(2)}) copy-start(f32[1,1024]{1,0:T(1,128)S(1)} %convert_element_type.471) | copy-start | bytes 12292
  72.3 159.1 %copy-start.55 = (f32[1,1024]{1,0:T(1,128)}, f32[1,1024]{1,0:T(1,128)S(1)}, u32[]{:S(2)}) copy-start(f32[1,1024]{1,0:T(1,128)S(1)} %convert_element_type.472) | copy-start | bytes 12292
  567.0 224.7 %copy-start.61 = (f32[1,1024]{1,0:T(1,128)S(1)}, f32[1,1024]{1,0:T(1,128)}, u32[]{:S(2)}) copy-start(f32[1,1024]{1,0:T(1,128)} %convert_element_type.478) | copy-start | bytes 12292
  1442.5 86.5 %copy-start.7 = (f32[64,77]{1,0:T(8,128)S(1)}, f32[64,77]{1,0:T(8,128)}, u32[]{:S(2)}) copy-start(f32[64,77]{1,0:T(8,128)} %copy-done.6) | copy-start | bytes 59140
  1442.5 86.5 %copy-start.13 = (f32[64,77]{1,0:T(8,128)S(1)}, f32[64,77]{1,0:T(8,128)}, u32[]{:S(2)}) copy-start(f32[64,77]{1,0:T(8,128)} %copy-done.12) | copy-start | bytes 59140
  1442.5 86.5 %copy-start.33 = (f32[1,1024]{1,0:T(1,128)S(1)}, f32[1,1024]{1,0:T(1,128)}, u32[]{:S(2)}) copy-start(f32[1,1024]{1,0:T(1,128)} %convert_element_type.483) | copy-start | bytes 12292
  1912.3 70.1 %copy-start.19 = (f32[64,77]{1,0:T(8,128)S(1)}, f32[64,77]{1,0:T(8,128)}, u32[]{:S(2)}) copy-start(f32[64,77]{1,0:T(8,128)} %copy-done.18) | copy-start | bytes 59140
  1912.3 70.1 %copy-start.25 = (f32[64,77]{1,0:T(8,128)S(1)}, f32[64,77]{1,0:T(8,128)}, u32[]{:S(2)}) copy-start(f32[64,77]{1,0:T(8,128)} %copy-done.24) | copy-start | bytes 59140
  1912.3 70.1 %copy-start.43 = (f32[1,1024]{1,0:T(1,128)S(1)}, f32[1,1024]{1,0:T(1,128)}, u32[]{:S(2)}) copy-start(f32[1,1024]{1,0:T(1,128)} %convert_element_type.479) | copy-start | bytes 12292
  2049.2 79.2 %copy-start.10 = (f32[64,77]{1,0:T(8,128)S(1)}, f32[64,77]{1,0:T(8,128)}, u32[]{:S(2)}) copy-start(f32[64,77]{1,0:T(8,128)} %copy-done.9) | copy-start | bytes 59140
  2049.2 79.2 %copy-start.16 = (f32[64,77]{1,0:T(8,128)S(1)}, f32[64,77]{1,0:T(8,128)}, u32[]{:S(2)}) copy-start(f32[64,77]{1,0:T(8,128)} %copy-done.15) | copy-start | bytes 59140
  2049.2 79.2 %copy-start.30 = (f32[1,1024]{1,0:T(1,128)S(1)}, f32[1,1024]{1,0:T(1,128)}, u32[]{:S(2)}) copy-start(f32[1,1024]{1,0:T(1,128)} %convert_element_type.475) | copy-start | bytes 12292
  2336.7 696.7 %reduce-scatter.15.cloned.1.call-start = ((), (), s32[]{:S(2)}) async-start(), calls=%async_computation.11 | async-start | bytes 5242880 | tf_op jit(solution)/shard_map/reduce_scatter | solution.py:117
  2383.1 650.2 %reduce-scatter.9.cloned.1.call-start = ((), (), s32[]{:S(2)}) async-start(), calls=%async_computation.8 | async-start | bytes 15728640 | tf_op jit(solution)/shard_map/reduce_scatter | solution.py:117
  2551.1 70.2 %copy-start.22 = (f32[64,77]{1,0:T(8,128)S(1)}, f32[64,77]{1,0:T(8,128)}, u32[]{:S(2)}) copy-start(f32[64,77]{1,0:T(8,128)} %copy-done.21) | copy-start | bytes 59140
  2551.1 70.2 %copy-start.36 = (f32[64,77]{1,0:T(8,128)S(1)}, f32[64,77]{1,0:T(8,128)}, u32[]{:S(2)}) copy-start(f32[64,77]{1,0:T(8,128)} %copy-done.35) | copy-start | bytes 59140
  2551.1 70.2 %copy-start.54 = (f32[1,1024]{1,0:T(1,128)S(1)}, f32[1,1024]{1,0:T(1,128)}, u32[]{:S(2)}) copy-start(f32[1,1024]{1,0:T(1,128)} %copy-done.53) | copy-start | bytes 12292
  2551.1 70.2 %copy-start.56 = (f32[1,1024]{1,0:T(1,128)S(1)}, f32[1,1024]{1,0:T(1,128)}, u32[]{:S(2)}) copy-start(f32[1,1024]{1,0:T(1,128)} %copy-done.55) | copy-start | bytes 12292
  2621.3 67.6 %copy-start.20 = (f32[64,77]{1,0:T(8,128)S(1)}, f32[64,77]{1,0:T(8,128)}, u32[]{:S(2)}) copy-start(f32[64,77]{1,0:T(8,128)} %copy-done.18) | copy-start | bytes 59140
  2621.3 67.6 %copy-start.26 = (f32[64,77]{1,0:T(8,128)S(1)}, f32[64,77]{1,0:T(8,128)}, u32[]{:S(2)}) copy-start(f32[64,77]{1,0:T(8,128)} %copy-done.24) | copy-start | bytes 59140
  2621.3 67.6 %copy-start.44 = (f32[1,1024]{1,0:T(1,128)S(1)}, f32[1,1024]{1,0:T(1,128)}, u32[]{:S(2)}) copy-start(f32[1,1024]{1,0:T(1,128)} %convert_element_type.479) | copy-start | bytes 12292
  2688.8 344.5 %reduce-scatter.11.cloned.1.call-start = ((), (), s32[]{:S(2)}) async-start(), calls=%async_computation.9 | async-start | bytes 15728640 | tf_op jit(solution)/shard_map/reduce_scatter | solution.py:117
  2733.3 300.1 %reduce-scatter.21.cloned.1.call-start = ((), (), s32[]{:S(2)}) async-start(), calls=%async_computation.14 | async-start | bytes 20971520 | tf_op jit(solution)/shard_map/reduce_scatter | solution.py:117
  2787.1 328.2 %reduce-scatter.17.cloned.1.call-start = ((), (), s32[]{:S(2)}) async-start(), calls=%async_computation.12 | async-start | bytes 20971520 | tf_op jit(solution)/shard_map/reduce_scatter | solution.py:117
  2843.5 393.0 %reduce-scatter.19.cloned.1.call-start = ((), (), s32[]{:S(2)}) async-start(), calls=%async_computation.13 | async-start | bytes 20971520 | tf_op jit(solution)/shard_map/reduce_scatter | solution.py:117
  2900.4 457.3 %reduce-scatter.23.cloned.1.call-start = ((), (), s32[]{:S(2)}) async-start(), calls=%async_computation.15 | async-start | bytes 20971520 | tf_op jit(solution)/shard_map/reduce_scatter | solution.py:117
  2900.4 86.7 %copy-start.28 = (f32[3,16,64]{2,1,0:T(8,128)S(1)}, f32[3,16,64]{2,1,0:T(8,128)}, u32[]{:S(2)}) copy-start(f32[3,16,64]{2,1,0:T(8,128)} %get-tuple-element.112) | copy-start | bytes 36868
  2900.5 87.3 %copy-start.27 = (f32[3,16,64]{2,1,0:T(8,128)S(1)}, f32[3,16,64]{2,1,0:T(8,128)}, u32[]{:S(2)}) copy-start(f32[3,16,64]{2,1,0:T(8,128)} %get-tuple-element.114) | copy-start | bytes 36868
  2900.5 88.0 %copy-start.23 = (f32[64,77]{1,0:T(8,128)S(1)}, f32[64,77]{1,0:T(8,128)}, u32[]{:S(2)}) copy-start(f32[64,77]{1,0:T(8,128)} %copy-done.21) | copy-start | bytes 59140
  2900.5 88.0 %copy-start.37 = (f32[64,77]{1,0:T(8,128)S(1)}, f32[64,77]{1,0:T(8,128)}, u32[]{:S(2)}) copy-start(f32[64,77]{1,0:T(8,128)} %copy-done.35) | copy-start | bytes 59140
  2987.1 444.9 %all-reduce.22.cloned.1.call-start = ((), (), s32[]{:S(2)}) async-start(), calls=%async_computation.24 | async-start | bytes 212992
  3033.2 324.5 %copy-start.71 = (u32[8]{0:T(128)S(1)}, u32[8]{0:T(128)}, u32[]{:S(2)}) copy-start(u32[8]{0:T(128)} %constant.92) | copy-start | bytes 100
  3033.2 327.0 %copy-start.62 = (bf16[1,256]{1,0:T(2,128)(2,1)S(1)}, bf16[1,256]{1,0:T(2,128)(2,1)}, u32[]{:S(2)}) copy-start(bf16[1,256]{1,0:T(2,128)(2,1)} %get-tuple-element.139) | copy-start | bytes 1540
  3033.2 912.5 %all-reduce.24.cloned.1.call-start = ((), (), s32[]{:S(2)}) async-start(), calls=%async_computation.25 | async-start | bytes 50331648 | tf_op jit(solution)/shard_map/psum | solution.py:117
  (46 other events, 1566.8 us)
Sparse Core Ops, SparseCore 0:
  12.6 46.4 all-gather.32
  60.6 19.9 all-gather.34
  82.7 56.5 all-gather.36
  141.3 56.5 all-gather.38
  199.8 43.5 all-gather.40
  244.8 19.5 all-gather.42
  266.5 55.7 all-gather.44
  324.3 55.7 all-gather.46
  2336.8 38.5 reduce-scatter.12
  2383.2 38.5 reduce-scatter.14
  2689.0 90.7 reduce-scatter.8
  2782.2 90.5 reduce-scatter.10
  2875.4 118.7 reduce-scatter.20
  2996.5 118.7 reduce-scatter.16
  3117.7 118.7 reduce-scatter.18
  3238.9 118.7 reduce-scatter.22
  3362.1 27.9 all-reduce.21
  3392.9 552.7 all-reduce.23
where the time goes:
time: 3990 us; the launch traced here: 3970 us
  matrix products  1940 us (49%)
  waiting for transfers between devices  815 us (20%)
  local copies, waits for them, and re-layouts  736 us (18%)
  other arithmetic  331 us (8%)
  blocking collectives  133 us (3%)
    psum x1, waiting for transfers between devices, reduce_grads(): lax.psum(lax.psum_scatter(grad, 'fsdp', scatter_dimension=0, tiled=True),...  488 us
    dot_general x2, matrix products, block_fwd(): jnp.einsum('btw,wf->btf', normed2, fc_weight, preferred_element_type=jnp....  449 us
    reduce_scatter x8, waiting for transfers between devices, reduce_grads(): lax.psum_scatter(grad, 'fsdp', scatter_dimension=0, tiled=True)  324 us
    reshape x4, local copies, waits for them, and re-layouts, attn_bwd(): return d_qkv.reshape(qkv.shape)  289 us
    unnamed x176, local copies, waits for them, and re-layouts  188 us
    dot_general x2, matrix products, block_bwd(): jnp.einsum('btw,fw->btf', d_result, proj_weight, preferred_element_type=j...  166 us
    dot_general x2, matrix products, block_bwd(): jnp.einsum('btf,btw->fw', hidden, d_result, preferred_element_type=jnp.fl...  140 us
    reshape x2, local copies, waits for them, and re-layouts, split_qkv(): grouped = qkv.reshape(qkv.shape[0], qkv.shape[1], 3, heads, HEAD_DIM)  134 us
  transfers between devices with their start and end apart: 18, of which 4 were waited for; matrix products, arithmetic and copies ran while one was open for 52% of the time, Pallas kernels for 0%

commit v1 on v0

v1 whole, which is shorter than its diff:
```python
import functools
import math

import jax
import jax.numpy as jnp
from jax import lax
from jax.experimental import pallas as pl
from jax.experimental.pallas import tpu as pltpu
from jax.sharding import PartitionSpec as P

HEAD_DIM = 64
NORM_EPS = 1e-5
RANKS = (2, 2, 3, 2, 3, 2, 2, 2, 3, 2, 3, 2)
BIG = (2, 4, 8, 10)
SMALL = (0, 1, 3, 5, 6, 7, 9, 11)
F32 = jnp.float32
BF16 = jnp.bfloat16
NT = (((1,), (1,)), ((), ()))
NN = (((1,), (0,)), ((), ()))
TN = (((0,), (0,)), ((), ()))
EXP_SCALE = math.log2(math.e) / 8.0


def mm(lhs, rhs, dims):
    return lax.dot_general(lhs, rhs, dims, preferred_element_type=F32)


def pair_masks(length):
    lane = lax.broadcasted_iota(jnp.int32, (length, 128), 1) < HEAD_DIM
    query = lax.broadcasted_iota(jnp.int32, (length, 256), 1) & 127
    key = lax.broadcasted_iota(jnp.int32, (length, 256), 0)
    return lane, key <= query


def attn_fwd_kernel(qkv_ref, out_ref, q_blocks, score_buf):
    captions, length, width = out_ref.shape

    @pl.when(pl.program_id(0) == 0)
    def _():
        q_blocks[...] = jnp.zeros_like(q_blocks)

    lane, causal = pair_masks(length)
    zero = jnp.zeros((length, 128), BF16)

    def caption(index, carry):
        for pair in range(width // 128):
            query = qkv_ref[index, :, 128 * pair:128 * pair + 128]
            q_blocks[pair, 0:length] = jnp.where(lane, query, zero)
            q_blocks[pair, 128:128 + length] = jnp.where(lane, zero, query)
        for pair in range(width // 128):
            keys = qkv_ref[index, :, width + 128 * pair:width + 128 * pair + 128]
            score_buf[pair] = mm(keys, q_blocks[pair], NT)
        for pair in range(width // 128):
            values = qkv_ref[index, :, 2 * width + 128 * pair:2 * width + 128 * pair + 128]
            scores = jnp.where(causal, score_buf[pair], -1e30)
            weights = jnp.exp2((scores - jnp.max(scores, axis=0, keepdims=True)) * EXP_SCALE)
            probs = (weights * (1.0 / jnp.sum(weights, axis=0, keepdims=True))).astype(BF16)
            both = mm(probs, values, TN)
            out_ref[index, :, 128 * pair:128 * pair + 128] = jnp.where(lane, both[0:length], both[128:128 + length]).astype(BF16)
        return carry

    lax.fori_loop(0, captions, caption, 0)


def attn_bwd_kernel(qkv_ref, d_out_ref, d_qkv_ref, q_blocks, d_blocks, score_buf, d_prob_buf):
    captions, length, width = d_out_ref.shape

    @pl.when(pl.program_id(0) == 0)
    def _():
        q_blocks[...] = jnp.zeros_like(q_blocks)
        d_blocks[...] = jnp.zeros_like(d_blocks)

    lane, causal = pair_masks(length)
    zero = jnp.zeros((length, 128), BF16)

    def caption(index, carry):
        for pair in range(width // 128):
            at = 128 * pair
            query = qkv_ref[index, :, at:at + 128]
            d_out = d_out_ref[index, :, at:at + 128]
            q_blocks[pair, 0:length] = jnp.where(lane, query, zero)
            q_blocks[pair, 128:128 + length] = jnp.where(lane, zero, query)
            d_blocks[pair, 0:length] = jnp.where(lane, d_out, zero)
            d_blocks[pair, 128:128 + length] = jnp.where(lane, zero, d_out)
        for pair in range(width // 128):
            at = 128 * pair
            score_buf[pair] = mm(qkv_ref[index, :, width + at:width + at + 128], q_blocks[pair], NT)
            d_prob_buf[pair] = mm(qkv_ref[index, :, 2 * width + at:2 * width + at + 128], d_blocks[pair], NT)
        for pair in range(width // 128):
            at = 128 * pair
            keys = qkv_ref[index, :, width + at:width + at + 128]
            scores = jnp.where(causal, score_buf[pair], -1e30)
            d_probs = d_prob_buf[pair].astype(BF16).astype(F32)
            weights = jnp.exp2((scores - jnp.max(scores, axis=0, keepdims=True)) * EXP_SCALE)
            probs = weights * (1.0 / jnp.sum(weights, axis=0, keepdims=True))
            inner = jnp.sum(probs * d_probs, axis=0, keepdims=True)
            d_scores = (probs * ((d_probs - inner) * (HEAD_DIM ** -0.5))).astype(BF16)
            d_query = mm(d_scores, keys, TN)
            d_qkv_ref[index, :, at:at + 128] = jnp.where(lane, d_query[0:length], d_query[128:128 + length]).astype(BF16)
            d_qkv_ref[index, :, width + at:width + at + 128] = mm(d_scores, q_blocks[pair], NN).astype(BF16)
            d_qkv_ref[index, :, 2 * width + at:2 * width + at + 128] = mm(probs.astype(BF16), d_blocks[pair], NN).astype(BF16)
        return carry

    lax.fori_loop(0, captions, caption, 0)


def attn_call(kernel, name, out_width, operands, flops):
    captions, length, _ = operands[0].shape
    width = operands[0].shape[2] // 3
    step = 4
    blocks = pltpu.VMEM((width // 128, 256, 128), BF16)
    scores = pltpu.VMEM((width // 128, length, 256), F32)
    copies = len(operands)
    return pl.pallas_call(
        kernel,
        grid=(captions // step,),
        in_specs=[pl.BlockSpec((step, length, x.shape[2]), lambda i: (i, 0, 0)) for x in operands],
        out_specs=pl.BlockSpec((step, length, out_width), lambda i: (i, 0, 0)),
        out_shape=jax.ShapeDtypeStruct((captions, length, out_width), BF16),
        scratch_shapes=[blocks] * copies + [scores] * copies,
        compiler_params=pltpu.CompilerParams(dimension_semantics=("arbitrary",), vmem_limit_bytes=48 * 2**20),
        cost_estimate=pl.CostEstimate(flops=flops, transcendentals=0, bytes_accessed=sum(2 * x.size for x in operands)),
        name=name,
    )(*operands)


def attn_fwd(qkv, length):
    rows, wide = qkv.shape
    by_caption = qkv.reshape(length, rows // length, wide).transpose(1, 0, 2)
    context = attn_call(attn_fwd_kernel, "attn_fwd", wide // 3, (by_caption,), 40 * 10**9)
    return context.transpose(1, 0, 2).reshape(rows, wide // 3), by_caption


def attn_bwd(d_context, by_caption, length):
    rows, width = d_context.shape
    d_by_caption = d_context.reshape(length, rows // length, width).transpose(1, 0, 2)
    d_qkv = attn_call(attn_bwd_kernel, "attn_bwd", 3 * width, (by_caption, d_by_caption), 60 * 10**9)
    return d_qkv.transpose(1, 0, 2).reshape(rows, 3 * width)


def norm_stats(source):
    src32 = source.astype(F32)
    centered = src32 - jnp.mean(src32, axis=-1, keepdims=True)
    inv_std = lax.rsqrt(jnp.mean(centered * centered, axis=-1, keepdims=True) + NORM_EPS)
    return centered * inv_std, inv_std


def norm_fwd(source, gain, shift):
    normed, _ = norm_stats(source)
    return (normed * gain + shift).astype(BF16)


def norm_bwd(d_out, source, gain, want_input):
    normed, inv_std = norm_stats(source)
    d_gain = jnp.sum(d_out * normed, axis=0)
    d_shift = jnp.sum(d_out, axis=0)
    if not want_input:
        return None, d_gain, d_shift
    d_norm = d_out * gain
    d_source = inv_std * (d_norm - jnp.mean(d_norm, axis=-1, keepdims=True) - normed * jnp.mean(d_norm * normed, axis=-1, keepdims=True))
    return d_source, d_gain, d_shift


def gelu_cdf(pre_act):
    return 0.5 * (1.0 + lax.erf(pre_act * 0.7071067811865476))


def gelu_grad(pre_act):
    return gelu_cdf(pre_act) + pre_act * jnp.exp(-0.5 * pre_act * pre_act) * 0.3989422804014327


def block_fwd(tokens, big, small, length):
    qkv_weight, out_weight, fc_weight, proj_weight = big
    ln1_gain, ln1_shift, qkv_bias, out_bias, ln2_gain, ln2_shift, fc_bias, proj_bias = small
    normed1 = norm_fwd(tokens, ln1_gain, ln1_shift)
    qkv = (mm(normed1, qkv_weight, NN) + qkv_bias).astype(BF16)
    context, by_caption = attn_fwd(qkv, length)
    middle = (tokens.astype(F32) + mm(context, out_weight, NN) + out_bias).astype(BF16)
    normed2 = norm_fwd(middle, ln2_gain, ln2_shift)
    pre_act = mm(normed2, fc_weight, NN) + fc_bias
    hidden = (pre_act * gelu_cdf(pre_act)).astype(BF16)
    result = (middle.astype(F32) + mm(hidden, proj_weight, NN) + proj_bias).astype(BF16)
    return result, (tokens, normed1, by_caption, context, middle, normed2, pre_act, hidden)


def block_bwd(d_result, saved, big, small, length, want_input, reduce_grad):
    qkv_weight, out_weight, fc_weight, proj_weight = big
    ln1_gain, _, _, _, ln2_gain, _, _, _ = small
    tokens, normed1, by_caption, context, middle, normed2, pre_act, hidden = saved
    d_res32 = d_result.astype(F32)
    g_proj_bias = jnp.sum(d_res32, axis=0)
    g_proj_weight = mm(hidden, d_result, TN)
    d_result, g_proj_weight = lax.optimization_barrier((d_result, g_proj_weight))
    r_proj = reduce_grad(g_proj_weight)
    d_hidden = mm(d_result, proj_weight, NT).astype(BF16).astype(F32)
    d_pre = d_hidden * gelu_grad(pre_act)
    g_fc_bias = jnp.sum(d_pre, axis=0)
    d_pre = d_pre.astype(BF16)
    g_fc_weight = mm(normed2, d_pre, TN)
    d_pre, g_fc_weight = lax.optimization_barrier((d_pre, g_fc_weight))
    r_fc = reduce_grad(g_fc_weight)
    d_normed2 = mm(d_pre, fc_weight, NT).astype(BF16).astype(F32)
    d_mid_norm, g_ln2_gain, g_ln2_shift = norm_bwd(d_normed2, middle, ln2_gain, True)
    d_middle = (d_res32 + d_mid_norm).astype(BF16)
    g_out_bias = jnp.sum(d_middle, axis=0, dtype=F32)
    g_out_weight = mm(context, d_middle, TN)
    d_middle, g_out_weight = lax.optimization_barrier((d_middle, g_out_weight))
    r_out = reduce_grad(g_out_weight)
    d_context = mm(d_middle, out_weight, NT).astype(BF16)
    d_qkv = attn_bwd(d_context, by_caption, length)
    g_qkv_bias = jnp.sum(d_qkv, axis=0, dtype=F32)
    g_qkv_weight = mm(normed1, d_qkv, TN)
    d_qkv, g_qkv_weight = lax.optimization_barrier((d_qkv, g_qkv_weight))
    r_qkv = reduce_grad(g_qkv_weight)
    d_normed1 = mm(d_qkv, qkv_weight, NT).astype(BF16).astype(F32)
    d_tok_norm, g_ln1_gain, g_ln1_shift = norm_bwd(d_normed1, tokens, ln1_gain, want_input)
    d_tokens = None
    if want_input:
        d_tokens = (d_middle.astype(F32) + d_tok_norm).astype(BF16)
    small_grads = (g_ln1_gain, g_ln1_shift, g_qkv_bias, g_out_bias, g_ln2_gain, g_ln2_shift, g_fc_bias, g_proj_bias)
    return d_tokens, (r_qkv, r_out, r_fc, r_proj), small_grads


def solution(mesh):
    batch_spec = P(('dp', 'fsdp'), None, None)
    param_specs = tuple(P(None, 'fsdp', None) if rank == 3 else P(None, 'fsdp') for rank in RANKS)
    shards = mesh.shape['fsdp']
    copies = mesh.shape['dp']
    swap = [(i, (i + 1) % copies) for i in range(copies)]

    def reduce_grad(grad):
        own = lax.psum_scatter(grad, 'fsdp', scatter_dimension=0, tiled=True)
        return own, lax.ppermute(own, 'dp', swap)

    def per_device(tokens, grad_out, *params):
        captions, length, width = tokens.shape
        rows = captions * length
        small_sizes = [params[i].shape[1] for i in SMALL]
        small_all = lax.all_gather(jnp.concatenate([params[i].astype(BF16) for i in SMALL], axis=1), 'fsdp', axis=0, tiled=False)

        def small_of(layer):
            found, at = [], 0
            for size in small_sizes:
                found.append(small_all[:, layer, at:at + size].reshape(-1).astype(F32))
                at += size
            return tuple(found)

        def big_of(layer):
            return tuple(lax.all_gather(params[i][layer].astype(BF16), 'fsdp', axis=0, tiled=True) for i in BIG)

        big0, big1 = big_of(0), big_of(1)
        small0, small1 = small_of(0), small_of(1)
        flat = tokens.transpose(1, 0, 2).reshape(rows, width)
        d_flat = grad_out.transpose(1, 0, 2).reshape(rows, width)
        mid_tokens, saved0 = block_fwd(flat, big0, small0, length)
        block_out, saved1 = block_fwd(mid_tokens, big1, small1, length)
        d_mid, wide1, narrow1 = block_bwd(d_flat, saved1, big1, small1, length, True, reduce_grad)
        _, wide0, narrow0 = block_bwd(d_mid, saved0, big0, small0, length, False, reduce_grad)

        split = [[grad.reshape(shards, 1, -1) for grad in narrow] for narrow in (narrow0, narrow1)]
        packed = jnp.concatenate([jnp.concatenate(row, axis=2) for row in split], axis=1)
        summed = lax.psum(packed, ('dp', 'fsdp'))
        mine = lax.dynamic_index_in_dim(summed, lax.axis_index('fsdp'), 0, keepdims=False)
        grads = [None] * len(RANKS)
        at = 0
        for i, size in zip(SMALL, small_sizes):
            grads[i] = mine[:, at:at + size]
            at += size
        for i, first, second in zip(BIG, wide0, wide1):
            grads[i] = jnp.stack([first[0] + first[1], second[0] + second[1]])
        block_out = block_out.reshape(length, captions, width).transpose(1, 0, 2)
        return (block_out,) + tuple(grads)

    return jax.shard_map(per_device, mesh=mesh, in_specs=(batch_spec, batch_spec) + param_specs, out_specs=(batch_spec,) + param_specs, check_vma=False)
```

time: 3990 us -> 2270 us (0.57)
  matrix products: 1940 us -> 1060 us
  local copies, waits for them, and re-layouts: 736 us -> 197 us
  waiting for transfers between devices: 815 us -> 559 us
  Pallas kernels: 0 us -> 225 us
  other arithmetic: 331 us -> 175 us
  blocking collectives: 133 us -> 10.5 us
    dot_general x36 -> x24, matrix products: 1940 us -> 1060 us  [mm(): return lax.dot_general(lhs, rhs, dims, preferred_element_type=F32)]
    psum x1, waiting for transfers between devices: 488 us -> 44.3 us  [per_device(): summed = lax.psum(packed, ('dp', 'fsdp'))]
    reshape x8 -> x4, local copies, waits for them, and re-layouts: 460 us -> 85.4 us  [the longest x2 58.5 us: attn_fwd(): by_caption = qkv.reshape(length, rows // length, wide).transpose(1, 0, 2)]
    pallas_call x0 -> x4, Pallas kernels: none -> 225 us  [attn_call(): pl.pallas_call(kernel, grid=(captions // step,), in_specs=[pl.BlockSpec((...]
    unnamed x176 -> x166, local copies, waits for them, and re-layouts: 188 us -> 15.5 us
    reduce_scatter x8, waiting for transfers between devices: 324 us -> 439 us  [reduce_grad(): own = lax.psum_scatter(grad, 'fsdp', scatter_dimension=0, tiled=True)]
    all_gather x16 -> x1, blocking collectives: 124 us -> 10.5 us  [per_device(): lax.all_gather(jnp.concatenate([params[i].astype(BF16) for i in SMALL], a...]
    sub x2 -> x0, other arithmetic: 95.6 us -> none  [attn_fwd(): probs = jax.nn.softmax(jnp.where(causal, scores, -1e+30), axis=-1)]
  transfers between devices with their start and end apart: 18 -> 25, of which waited for: 4 -> 7; matrix products, arithmetic and copies ran while one was open for 52% -> 37% of each run, Pallas kernels for 0% -> 7%
where the time goes in v1:
time: 2270 us; the launch traced here: 2260 us
  matrix products  1060 us (47%)
  waiting for transfers between devices  559 us (25%)
  Pallas kernels  225 us (10%)
  local copies, waits for them, and re-layouts  197 us (9%)
  other arithmetic  175 us (8%)
    dot_general x24, matrix products, mm(): return lax.dot_general(lhs, rhs, dims, preferred_element_type=F32)  1060 us
    reduce_scatter x8, waiting for transfers between devices, reduce_grad(): own = lax.psum_scatter(grad, 'fsdp', scatter_dimension=0, tiled=True)  439 us
    pallas_call x4, Pallas kernels, attn_call(): pl.pallas_call(kernel, grid=(captions // step,), in_specs=[pl.BlockSpec((...  225 us
    ppermute x8, waiting for transfers between devices, reduce_grad(): return (own, lax.ppermute(own, 'dp', swap))  70.5 us
    reshape x2, local copies, waits for them, and re-layouts, attn_fwd(): by_caption = qkv.reshape(length, rows // length, wide).transpose(1, 0, 2)  58.5 us
    transpose x2, local copies, waits for them, and re-layouts, attn_bwd(): return d_qkv.transpose(1, 0, 2).reshape(rows, 3 * width)  58.3 us
  transfers between devices with their start and end apart: 25, of which 7 were waited for; matrix products, arithmetic and copies ran while one was open for 37% of the time, Pallas kernels for 7%

profile of v1, /device:TPU:0, one launch (start us, length us, event | category | flops | bytes accessed | tf_op | source)
XLA Modules:
  0.0 2259.3 jit_solution(333459895922703686)
XLA Ops:
  65.4 39.9 %add_convert_fusion.1 = bf16[4928,3072]{1,0:T(8,128)(2,1)} fusion(bf16[4928,1024]{1,0:T(8,128)(2,1)} %fusion.75, f32[3072]{0:T(1024)S(1)} %bitcast.273, bf16[1,1024,3072]{2,1,0:T(8,128)(2,1)} %all-gather.19.cloned.1.call-done), kind=kOutput, calls=%fused_computation.19 | convolution fusion | flops 31034572800 | bytes 46673920 | tf_op jit(solution)/shard_map/dot_general | solution.py:25
  105.2 29.2 %copy.51 = bf16[77,64,3072]{2,0,1:T(8,128)(2,1)} copy(bf16[77,64,3072]{2,1,0:T(8,128)(2,1)} %bitcast.227) | data formatting | bytes 60555264 | tf_op jit(solution)/shard_map/reshape | solution.py:129
  134.5 46.0 %attn_fwd.2 = bf16[64,77,1024]{2,1,0:T(8,128)(2,1)} custom-call(bf16[64,77,3072]{2,1,0:T(8,128)(2,1)} %bitcast.220), custom_call_target="tpu_custom_call" | custom-call | flops 40000000000 | bytes 30277632 | tf_op jit(solution)/shard_map/attn_fwd/pallas_call | solution.py:114
  180.5 13.7 copy.38
  194.2 17.4 fusion.83
  222.5 60.9 %multiply_convert_fusion.1 = (bf16[4928,4096]{1,0:T(8,128)(2,1)}, f32[4928,4096]{1,0:T(8,128)}) fusion(f32[4096]{0:T(1024)S(1)} %bitcast.259, bf16[1,1024,4096]{2,1,0:T(8,128)(2,1)} %all-gather.23.cloned.1.call-done, bf16[4928,1024]{1,0:T(8,128)(2,1)} %copy-done, f32[1024]{0:T(1024)S(1)} %bitcast.270, f32[1024]{0:T(1024)S(1)} %bitcast.242, ...), kind=kOutput, calls=%fused_computation.14 | convolution fusion | flops 41490448384 | bytes 139655680 | tf_op jit(solution)/shard_map/dot_general | solution.py:25
  283.4 51.8 %convert_reduce_fusion.6 = (f32[4928]{0:T(1024)S(1)}, bf16[4928,1024]{1,0:T(8,128)(2,1)S(1)}) fusion(f32[1024]{0:T(1024)S(1)} %bitcast.278, bf16[4928,4096]{1,0:T(8,128)(2,1)} %get-tuple-element.99, bf16[1,4096,1024]{2,1,0:T(8,128)(2,1)} %all-gather.25.cloned.1.call-done, bf16[4928,1024]{1,0:T(8,128)(2,1)} %copy-done), kind=kOutput, calls=%fused_computation.36 | convolution fusion | flops 41369333760 | bytes 68967680 | tf_op jit(solution)/shard_map/dot_general | solution.py:25
  341.9 40.4 %add_convert_fusion = bf16[4928,3072]{1,0:T(8,128)(2,1)} fusion(f32[3072]{0:T(1024)S(1)} %bitcast.272, bf16[1,1024,3072]{2,1,0:T(8,128)(2,1)} %all-gather.27.cloned.1.call-done, bf16[4928,1024]{1,0:T(8,128)(2,1)} %copy-done.3, f32[1024]{0:T(1024)S(1)} %bitcast.275, f32[1024]{0:T(1024)S(1)} %bitcast.249, f32[4928]{0:T(1024)S(1)} %add_rsqrt_fusion.2, ...), kind=kOutput, calls=%fused_computation.18 | convolution fusion | flops 31064850432 | bytes 46721536 | tf_op jit(solution)/shard_map/dot_general | solution.py:25
  382.3 29.2 %copy.50 = bf16[77,64,3072]{2,0,1:T(8,128)(2,1)} copy(bf16[77,64,3072]{2,1,0:T(8,128)(2,1)} %bitcast.228) | data formatting | bytes 60555264 | tf_op jit(solution)/shard_map/reshape | solution.py:129
  411.5 46.0 %attn_fwd.3 = bf16[64,77,1024]{2,1,0:T(8,128)(2,1)} custom-call(bf16[64,77,3072]{2,1,0:T(8,128)(2,1)} %bitcast.222), custom_call_target="tpu_custom_call" | custom-call | flops 40000000000 | bytes 30277632 | tf_op jit(solution)/shard_map/attn_fwd/pallas_call | solution.py:114
  457.5 13.6 copy.40
  471.2 20.5 convert_reduce_fusion.5
  498.5 61.4 %multiply_convert_fusion = (bf16[4928,4096]{1,0:T(8,128)(2,1)}, f32[4928,4096]{1,0:T(8,128)}) fusion(f32[4096]{0:T(1024)S(1)} %bitcast.261, bf16[1,1024,4096]{2,1,0:T(8,128)(2,1)} %all-gather.31.cloned.1.call-done, bf16[4928,1024]{1,0:T(8,128)(2,1)} %get-tuple-element.104, f32[1024]{0:T(1024)S(1)} %bitcast.267, f32[1024]{0:T(1024)S(1)} %bitcast.245, ...), kind=kOutput, calls=%fused_computation.12 | convolution fusion | flops 41490448384 | bytes 139655680 | tf_op jit(solution)/shard_map/dot_general | solution.py:25
  559.9 53.5 %fusion.124 = f32[4096,1024]{1,0:T(8,128)} fusion(bf16[4928,4096]{1,0:T(8,128)(2,1)} %get-tuple-element.105, bf16[4928,1024]{1,0:T(8,128)(2,1)} %bitcast.218), kind=kOutput, calls=%fused_computation.228 | convolution fusion | flops 41339060224 | bytes 67239936 | tf_op jit(solution)/shard_map/dot_general | solution.py:25
  613.4 11.4 fusion.158
  624.8 82.8 %fusion.118 = (f32[4096]{0:T(1024)}, bf16[4928,4096]{1,0:T(8,128)(2,1)}) fusion(f32[4928,4096]{1,0:T(8,128)} %get-tuple-element.106, f32[4096]{0:T(1024)S(1)} %bitcast.262, bf16[4928,1024]{1,0:T(8,128)(2,1)} %bitcast.219, bf16[1,4096,1024]{2,1,0:T(8,128)(2,1)} %all-gather.33.cloned.1.call-done), kind=kOutput, calls=%fused_computation.222 | convolution fusion | flops 41621647360 | bytes 139624448 | tf_op jit(solution)/shard_map/dot_general | solution.py:25
  707.6 53.8 %fusion.111 = f32[1024,4096]{1,0:T(8,128)} fusion(bf16[4928,4096]{1,0:T(8,128)(2,1)} %get-tuple-element.30, bf16[4928,1024]{1,0:T(8,128)(2,1)} %fusion.158), kind=kOutput, calls=%fused_computation.220 | convolution fusion | flops 41339060224 | bytes 67239936 | tf_op jit(solution)/shard_map/dot_general | solution.py:25
  761.4 57.8 %fusion.61 = (f32[1024]{0:T(1024)}, f32[4928]{0:T(1024)S(1)}, f32[4928]{0:T(1024)S(1)}, f32[1024]{0:T(1024)}, bf16[4928,1024]{1,0:T(8,128)(2,1)}) fusion(bf16[4928,1024]{1,0:T(8,128)(2,1)} %get-tuple-element.104, f32[4928]{0:T(1024)S(1)} %copy-done.25, f32[4928]{0:T(1024)S(1)} %copy-done.19, f32[1024]{0:T(1024)S(1)} %bitcast.247, ...), kind=kOutput, calls=%fused_computation.95 | convolution fusion | flops 41399607296 | bytes 69035008 | tf_op jit(solution)/shard_map/dot_general | solution.py:25
  819.2 15.1 convert_reduce_fusion.11
  838.0 12.6 fusion.125
  850.6 17.0 convolution_convert_fusion.4
  867.6 13.4 copy.53
  881.1 66.7 %attn_bwd.2 = bf16[64,77,3072]{2,1,0:T(8,128)(2,1)} custom-call(bf16[64,77,3072]{2,1,0:T(8,128)(2,1)} %bitcast.223, bf16[64,77,1024]{2,1,0:T(8,128)(2,1)} %bitcast.229), custom_call_target="tpu_custom_call" | custom-call | flops 60000002048 | bytes 40370176 | tf_op jit(solution)/shard_map/attn_bwd/pallas_call | solution.py:114
  947.8 29.1 %copy.42 = bf16[77,64,3072]{2,1,0:T(8,128)(2,1)} copy(bf16[77,64,3072]{2,0,1:T(8,128)(2,1)} %bitcast.216) | data formatting | bytes 60555264 | tf_op jit(solution)/shard_map/transpose | solution.py:138
  976.9 44.6 %fusion.108 = f32[1024,3072]{1,0:T(8,128)} fusion(bf16[4928,3072]{1,0:T(8,128)(2,1)} %bitcast.225, bf16[4928,1024]{1,0:T(8,128)(2,1)} %copy-done.3, f32[1024]{0:T(1024)S(1)} %bitcast.276, f32[1024]{0:T(1024)S(1)} %bitcast.250, f32[4928]{0:T(1024)S(1)} %copy-done.29, f32[4928]{0:T(1024)S(1)} %copy-done.23), kind=kOutput, calls=%fused_computation.219 | convolution fusion | flops 31034572800 | bytes 53000704 | tf_op jit(solution)/shard_map/dot_general | solution.py:25
  1021.5 43.9 %fusion.53 = (f32[4928]{0:T(1024)S(1)}, f32[1024]{0:T(1024)}, f32[4928]{0:T(1024)S(1)}, f32[1024]{0:T(1024)}, bf16[4928,1024]{1,0:T(8,128)(2,1)}) fusion(bf16[4928,1024]{1,0:T(8,128)(2,1)} %copy-done.3, f32[1024]{0:T(1024)S(1)} %bitcast.251, f32[4928]{0:T(1024)S(1)} %copy-done.29, f32[4928]{0:T(1024)S(1)} %copy-done.23, bf16[4928,3072]{1,0:T(8,128)(2,1)} %bitcast.226, ...), kind=kOutput, calls=%fused_computation.87 | convolution fusion | flops 31064842240 | bytes 56845312 | tf_op jit(solution)/shard_map/dot_general | solution.py:25
  1065.5 14.3 convert_reduce_fusion.9
  1083.6 50.5 %fusion.126 = f32[4096,1024]{1,0:T(8,128)} fusion(bf16[4928,4096]{1,0:T(8,128)(2,1)} %get-tuple-element.99, bf16[4928,1024]{1,0:T(8,128)(2,1)S(1)} %get-tuple-element.33), kind=kOutput, calls=%fused_computation.230 | convolution fusion | flops 41339060224 | bytes 67239936 | tf_op jit(solution)/shard_map/dot_general | solution.py:25
  1134.1 83.1 %fusion.117 = (f32[4096]{0:T(1024)}, bf16[4928,4096]{1,0:T(8,128)(2,1)}) fusion(f32[4928,4096]{1,0:T(8,128)} %get-tuple-element.100, f32[4096]{0:T(1024)S(1)} %bitcast.260, bf16[4928,1024]{1,0:T(8,128)(2,1)} %copy-done.1, bf16[1,4096,1024]{2,1,0:T(8,128)(2,1)} %all-gather.25.cloned.1.call-done), kind=kOutput, calls=%fused_computation.221 | convolution fusion | flops 41621647360 | bytes 139624448 | tf_op jit(solution)/shard_map/dot_general | solution.py:25
  1217.2 53.5 %fusion.105 = f32[1024,4096]{1,0:T(8,128)} fusion(bf16[4928,4096]{1,0:T(8,128)(2,1)} %get-tuple-element.34, bf16[4928,1024]{1,0:T(8,128)(2,1)} %fusion.156), kind=kOutput, calls=%fused_computation.218 | convolution fusion | flops 41339060224 | bytes 67239936 | tf_op jit(solution)/shard_map/dot_general | solution.py:25
  1270.8 57.8 %fusion.63 = (f32[1024]{0:T(1024)}, f32[4928]{0:T(1024)S(1)}, f32[4928]{0:T(1024)S(1)}, f32[1024]{0:T(1024)}, bf16[4928,1024]{1,0:T(8,128)(2,1)}) fusion(bf16[4928,1024]{1,0:T(8,128)(2,1)} %copy-done, f32[4928]{0:T(1024)S(1)} %copy-done.21, f32[4928]{0:T(1024)S(1)} %copy-done.17, f32[1024]{0:T(1024)S(1)} %bitcast.243, ...), kind=kOutput, calls=%fused_computation.97 | convolution fusion | flops 41399607296 | bytes 69035008 | tf_op jit(solution)/shard_map/dot_general | solution.py:25
  1328.7 15.1 convert_reduce_fusion.12
  1347.6 12.6 fusion.127
  1361.0 17.1 convolution_convert_fusion.1
  1378.1 13.5 copy.52
  1391.6 66.7 %attn_bwd.3 = bf16[64,77,3072]{2,1,0:T(8,128)(2,1)} custom-call(bf16[64,77,3072]{2,1,0:T(8,128)(2,1)} %bitcast.221, bf16[64,77,1024]{2,1,0:T(8,128)(2,1)} %bitcast.230), custom_call_target="tpu_custom_call" | custom-call | flops 60000002048 | bytes 40370176 | tf_op jit(solution)/shard_map/attn_bwd/pallas_call | solution.py:114
  1458.3 29.2 %copy.44 = bf16[77,64,3072]{2,1,0:T(8,128)(2,1)} copy(bf16[77,64,3072]{2,0,1:T(8,128)(2,1)} %bitcast.217) | data formatting | bytes 60555264 | tf_op jit(solution)/shard_map/transpose | solution.py:138
  1487.5 44.6 %fusion.94 = f32[1024,3072]{1,0:T(8,128)} fusion(bf16[77,64,3072]{2,1,0:T(8,128)(2,1)} %copy.44, bf16[64,77,1024]{2,0,1:T(8,128)(2,1)} %param.14, f32[1024]{0:T(1024)S(1)} %bitcast.264, f32[1024]{0:T(1024)S(1)} %bitcast.266, f32[77,64]{1,0:T(8,128)S(1)} %copy-done.27, f32[77,64]{1,0:T(8,128)S(1)} %copy-done.15), kind=kOutput, calls=%fused_computation.143 | convolution fusion | flops 31034572800 | bytes 53000704 | tf_op jit(solution)/shard_map/dot_general | solution.py:25
  1539.1 37.9 %convert_reduce_fusion.8 = (f32[1024]{0:T(1024)S(1)}, f32[1024]{0:T(1024)S(1)}) fusion(f32[4928]{0:T(1024)S(1)} %copy-done.33, f32[4928]{0:T(1024)S(1)} %copy-done.31, bf16[64,77,1024]{2,0,1:T(8,128)(2,1)} %param.14, bf16[4928,3072]{1,0:T(8,128)(2,1)} %bitcast.224, bf16[1,1024,3072]{2,1,0:T(8,128)(2,1)} %all-gather.19.cloned.1.call-done), kind=kOutput, calls=%fused_computation.49 | convolution fusion | flops 31044665344 | bytes 46709248 | tf_op jit(solution)/shard_map/dot_general | solution.py:25
  1577.1 10.8 convert_reduce_fusion
  1604.5 18.3 reduce-scatter.9.cloned.1.call-done
  1624.3 119.8 %reduce-scatter.23.cloned.1.call-done = f32[1024,1024]{1,0:T(8,128)} async-done(((f32[4096,1024]{1,0:T(8,128)}), f32[1024,1024]{1,0:T(8,128)}) %reduce-scatter.23.cloned.1.call-update) | async-done | bytes 4194320 | tf_op jit(solution)/shard_map/reduce_scatter | solution.py:232
  1745.6 49.6 %fusion.60 = bf16[4928,1024]{1,0:T(8,128)(2,1)} fusion(bf16[4928,1024]{1,0:T(8,128)(2,1)} %get-tuple-element.104, bf16[4928,4096]{1,0:T(8,128)(2,1)} %get-tuple-element.105, f32[1024]{0:T(1024)S(1)} %bitcast.274, bf16[1,4096,1024]{2,1,0:T(8,128)(2,1)} %all-gather.33.cloned.1.call-done), kind=kOutput, calls=%fused_computation.94 | convolution fusion | flops 41359245312 | bytes 68947968 | tf_op jit(solution)/shard_map/dot_general | solution.py:25
  1795.2 70.1 %reduce-scatter.19.cloned.1.call-done = f32[256,4096]{1,0:T(8,128)} async-done(((f32[1024,4096]{1,0:T(8,128)}), f32[256,4096]{1,0:T(8,128)}) %reduce-scatter.19.cloned.1.call-update) | async-done | bytes 4194320 | tf_op jit(solution)/shard_map/reduce_scatter | solution.py:232
  1866.7 44.3 %all-reduce.2.cloned.1.call-done = f32[4,2,3328]{2,1,0:T(2,128)} async-done(((f32[4,2,3328]{2,1,0:T(2,128)}), f32[4,2,3328]{2,1,0:T(2,128)}) %all-reduce.2.cloned.1.call-update) | async-done | bytes 106512 | tf_op jit(solution)/shard_map/psum | solution.py:262
  1916.3 115.4 %reduce-scatter.17.cloned.1.call-done = f32[256,4096]{1,0:T(8,128)} async-done(((f32[1024,4096]{1,0:T(8,128)}), f32[256,4096]{1,0:T(8,128)}) %reduce-scatter.17.cloned.1.call-update) | async-done | bytes 4194320 | tf_op jit(solution)/shard_map/reduce_scatter | solution.py:232
  2037.8 115.0 %reduce-scatter.21.cloned.1.call-done = f32[1024,1024]{1,0:T(8,128)} async-done(((f32[4096,1024]{1,0:T(8,128)}), f32[1024,1024]{1,0:T(8,128)}) %reduce-scatter.21.cloned.1.call-update) | async-done | bytes 4194320 | tf_op jit(solution)/shard_map/reduce_scatter | solution.py:232
  2174.5 70.4 %collective-permute-done.6 = f32[1024,1024]{1,0:T(8,128)} collective-permute-done((f32[1024,1024]{1,0:T(8,128)}, f32[1024,1024]{1,0:T(8,128)}, u32[]{:S(2)}, u32[]{:S(2)}) %collective-permute-start.6) | collective-permute-done | bytes 4194336 | tf_op jit(solution)/shard_map/ppermute | solution.py:233
  (290 shorter events, 162.4 us)
Async XLA Ops:
  7.2 58.2 %all-gather.19.cloned.1.call-start = ((), (), s32[]{:S(2)}) async-start(), calls=%async_computation.17 | async-start | bytes 7864320 | tf_op jit(solution)/shard_map/all_gather | solution.py:249
  12.3 181.8 %all-gather.21.cloned.1.call-start = ((), (), s32[]{:S(2)}) async-start(), calls=%async_computation.18 | async-start | bytes 2621440 | tf_op jit(solution)/shard_map/all_gather | solution.py:249
  15.3 207.2 %all-gather.23.cloned.1.call-start = ((), (), s32[]{:S(2)}) async-start(), calls=%async_computation.19 | async-start | bytes 10485760 | tf_op jit(solution)/shard_map/all_gather | solution.py:249
  21.7 261.7 %all-gather.25.cloned.1.call-start = ((), (), s32[]{:S(2)}) async-start(), calls=%async_computation.20 | async-start | bytes 10485760 | tf_op jit(solution)/shard_map/all_gather | solution.py:249
  28.3 313.6 %all-gather.27.cloned.1.call-start = ((), (), s32[]{:S(2)}) async-start(), calls=%async_computation.21 | async-start | bytes 7864320 | tf_op jit(solution)/shard_map/all_gather | solution.py:249
  28.9 442.3 %all-gather.29.cloned.1.call-start = ((), (), s32[]{:S(2)}) async-start(), calls=%async_computation.22 | async-start | bytes 2621440 | tf_op jit(solution)/shard_map/all_gather | solution.py:249
  29.4 469.0 %all-gather.31.cloned.1.call-start = ((), (), s32[]{:S(2)}) async-start(), calls=%async_computation.23 | async-start | bytes 10485760 | tf_op jit(solution)/shard_map/all_gather | solution.py:249
  30.2 594.6 %all-gather.33.cloned.1.call-start = ((), (), s32[]{:S(2)}) async-start(), calls=%async_computation.24 | async-start | bytes 10485760 | tf_op jit(solution)/shard_map/all_gather | solution.py:249
  30.9 1570.1 %reduce-scatter.15.cloned.1.call-start = ((), (), s32[]{:S(2)}) async-start(), calls=%async_computation.12 | async-start | bytes 5242880 | tf_op jit(solution)/shard_map/reduce_scatter | solution.py:232
  48.8 56.4 %copy-start.14 = (f32[77,64]{1,0:T(8,128)}, f32[77,64]{1,0:T(8,128)S(1)}, u32[]{:S(2)}) copy-start(f32[77,64]{1,0:T(8,128)S(1)} %broadcast_multiply_fusion) | copy-start | bytes 59140
  55.6 49.7 %copy-start.30 = (f32[4928]{0:T(1024)}, f32[4928]{0:T(1024)S(1)}, u32[]{:S(2)}) copy-start(f32[4928]{0:T(1024)S(1)} %div.53) | copy-start | bytes 59140
  55.6 49.6 %copy-start.26 = (f32[77,64]{1,0:T(8,128)}, f32[77,64]{1,0:T(8,128)S(1)}, u32[]{:S(2)}) copy-start(f32[77,64]{1,0:T(8,128)S(1)} %add_rsqrt_fusion) | copy-start | bytes 59140
  213.1 70.3 %copy-start.16 = (f32[4928]{0:T(1024)}, f32[4928]{0:T(1024)S(1)}, u32[]{:S(2)}) copy-start(f32[4928]{0:T(1024)S(1)} %broadcast_multiply_fusion.9) | copy-start | bytes 59140
  215.9 67.4 %copy-start.20 = (f32[4928]{0:T(1024)}, f32[4928]{0:T(1024)S(1)}, u32[]{:S(2)}) copy-start(f32[4928]{0:T(1024)S(1)} %add_rsqrt_fusion.3) | copy-start | bytes 59140
  222.5 60.9 %copy-start.61 = (f32[4,1,256]{2,1,0:T(1,128)S(1)}, f32[4,1,256]{2,1,0:T(1,128)}, u32[]{:S(2)}) copy-start(f32[4,1,256]{2,1,0:T(1,128)} %get-tuple-element.83) | copy-start | bytes 12292
  283.4 58.5 %copy-start.38 = (f32[4,1,256]{2,1,0:T(1,128)S(1)}, f32[4,1,256]{2,1,0:T(1,128)}, u32[]{:S(2)}) copy-start(f32[4,1,256]{2,1,0:T(1,128)} %get-tuple-element.82) | copy-start | bytes 12292
  283.4 58.5 %copy-start.54 = (f32[4,1,768]{2,1,0:T(1,128)S(1)}, f32[4,1,768]{2,1,0:T(1,128)}, u32[]{:S(2)}) copy-start(f32[4,1,768]{2,1,0:T(1,128)} %get-tuple-element.91) | copy-start | bytes 36868
  283.4 58.5 %copy-start.58 = (f32[4,1,256]{2,1,0:T(1,128)S(1)}, f32[4,1,256]{2,1,0:T(1,128)}, u32[]{:S(2)}) copy-start(f32[4,1,256]{2,1,0:T(1,128)} %get-tuple-element.81) | copy-start | bytes 12292
  491.7 121.6 %copy-start.18 = (f32[4928]{0:T(1024)}, f32[4928]{0:T(1024)S(1)}, u32[]{:S(2)}) copy-start(f32[4928]{0:T(1024)S(1)} %broadcast_multiply_fusion.7) | copy-start | bytes 59140
  498.4 114.9 %copy-start.24 = (f32[4928]{0:T(1024)}, f32[4928]{0:T(1024)S(1)}, u32[]{:S(2)}) copy-start(f32[4928]{0:T(1024)S(1)} %add_rsqrt_fusion.1) | copy-start | bytes 59140
  707.6 53.8 %copy-start.19 = (f32[4928]{0:T(1024)S(1)}, f32[4928]{0:T(1024)}, u32[]{:S(2)}) copy-start(f32[4928]{0:T(1024)} %copy-done.18) | copy-start | bytes 59140
  707.6 53.8 %copy-start.25 = (f32[4928]{0:T(1024)S(1)}, f32[4928]{0:T(1024)}, u32[]{:S(2)}) copy-start(f32[4928]{0:T(1024)} %copy-done.24) | copy-start | bytes 59140
  707.6 53.8 %copy-start.37 = (f32[4,1,256]{2,1,0:T(1,128)S(1)}, f32[4,1,256]{2,1,0:T(1,128)}, u32[]{:S(2)}) copy-start(f32[4,1,256]{2,1,0:T(1,128)} %get-tuple-element.79) | copy-start | bytes 12292
  1083.6 50.5 %copy-start.46 = (f32[4,1,1024]{2,1,0:T(1,128)S(1)}, f32[4,1,1024]{2,1,0:T(1,128)}, u32[]{:S(2)}) copy-start(f32[4,1,1024]{2,1,0:T(1,128)} %get-tuple-element.90) | copy-start | bytes 49156
  1217.2 53.6 %copy-start.17 = (f32[4928]{0:T(1024)S(1)}, f32[4928]{0:T(1024)}, u32[]{:S(2)}) copy-start(f32[4928]{0:T(1024)} %copy-done.16) | copy-start | bytes 59140
  1217.2 53.6 %copy-start.21 = (f32[4928]{0:T(1024)S(1)}, f32[4928]{0:T(1024)}, u32[]{:S(2)}) copy-start(f32[4928]{0:T(1024)} %copy-done.20) | copy-start | bytes 59140
  1217.2 53.6 %copy-start.35 = (f32[4,1,256]{2,1,0:T(1,128)S(1)}, f32[4,1,256]{2,1,0:T(1,128)}, u32[]{:S(2)}) copy-start(f32[4,1,256]{2,1,0:T(1,128)} %get-tuple-element.85) | copy-start | bytes 12292
  1270.8 331.7 %reduce-scatter.13.cloned.1.call-start = ((), (), s32[]{:S(2)}) async-start(), calls=%async_computation.11 | async-start | bytes 5242880 | tf_op jit(solution)/shard_map/reduce_scatter | solution.py:232
  1360.2 242.8 %reduce-scatter.11.cloned.1.call-start = ((), (), s32[]{:S(2)}) async-start(), calls=%async_computation.10 | async-start | bytes 15728640 | tf_op jit(solution)/shard_map/reduce_scatter | solution.py:232
  1361.0 261.8 %reduce-scatter.9.cloned.1.call-start = ((), (), s32[]{:S(2)}) async-start(), calls=%async_computation.9 | async-start | bytes 15728640 | tf_op jit(solution)/shard_map/reduce_scatter | solution.py:232
  1532.1 212.0 %reduce-scatter.23.cloned.1.call-start = ((), (), s32[]{:S(2)}) async-start(), calls=%async_computation.16 | async-start | bytes 20971520 | tf_op jit(solution)/shard_map/reduce_scatter | solution.py:232
  1532.9 332.4 %reduce-scatter.19.cloned.1.call-start = ((), (), s32[]{:S(2)}) async-start(), calls=%async_computation.14 | async-start | bytes 20971520 | tf_op jit(solution)/shard_map/reduce_scatter | solution.py:232
  1533.5 377.6 %all-reduce.2.cloned.1.call-start = ((), (), s32[]{:S(2)}) async-start(), calls=%async_computation.8 | async-start | bytes 212992 | tf_op jit(solution)/shard_map/psum | solution.py:262
  1598.9 146.6 %copy-start.57 = (f32[4,1,256]{2,1,0:T(1,128)S(1)}, f32[4,1,256]{2,1,0:T(1,128)}, u32[]{:S(2)}) copy-start(f32[4,1,256]{2,1,0:T(1,128)} %get-tuple-element.77) | copy-start | bytes 12292
  1599.8 431.9 %reduce-scatter.17.cloned.1.call-start = ((), (), s32[]{:S(2)}) async-start(), calls=%async_computation.13 | async-start | bytes 20971520 | tf_op jit(solution)/shard_map/reduce_scatter | solution.py:232
  1600.4 552.5 %reduce-scatter.21.cloned.1.call-start = ((), (), s32[]{:S(2)}) async-start(), calls=%async_computation.15 | async-start | bytes 20971520 | tf_op jit(solution)/shard_map/reduce_scatter | solution.py:232
  1601.0 194.2 %collective-permute-start.3 = (f32[256,1024]{1,0:T(8,128)}, f32[256,1024]{1,0:T(8,128)S(1)}, u32[]{:S(2)}, u32[]{:S(2)}) collective-permute-start(f32[256,1024]{1,0:T(8,128)} %reduce-scatter.15.cloned.1.call-done), channel_id=1, source_target_pairs={{0,4},{4,0},{1,5},{5,1},{2,6},{6,2},{3,7},{7,3}} | collective-permute-start | bytes 3145736 | tf_op jit(solution)/shard_map/ppermute | solution.py:233
  1602.5 312.5 %collective-permute-start.2 = (f32[256,1024]{1,0:T(8,128)}, f32[256,1024]{1,0:T(8,128)}, u32[]{:S(2)}, u32[]{:S(2)}) collective-permute-start(f32[256,1024]{1,0:T(8,128)} %reduce-scatter.13.cloned.1.call-done), channel_id=1, source_target_pairs={{0,4},{4,0},{1,5},{5,1},{2,6},{6,2},{3,7},{7,3}} | collective-permute-start | bytes 3145736 | tf_op jit(solution)/shard_map/ppermute | solution.py:233
  1603.1 431.6 %collective-permute-start.1 = (f32[256,3072]{1,0:T(8,128)}, f32[256,3072]{1,0:T(8,128)}, u32[]{:S(2)}, u32[]{:S(2)}) collective-permute-start(f32[256,3072]{1,0:T(8,128)} %reduce-scatter.11.cloned.1.call-done), channel_id=1, source_target_pairs={{0,4},{4,0},{1,5},{5,1},{2,6},{6,2},{3,7},{7,3}} | collective-permute-start | bytes 9437192 | tf_op jit(solution)/shard_map/ppermute | solution.py:233
  1622.8 531.6 %collective-permute-start = (f32[256,3072]{1,0:T(8,128)}, f32[256,3072]{1,0:T(8,128)}, u32[]{:S(2)}, u32[]{:S(2)}) collective-permute-start(f32[256,3072]{1,0:T(8,128)} %reduce-scatter.9.cloned.1.call-done), channel_id=1, source_target_pairs={{0,4},{4,0},{1,5},{5,1},{2,6},{6,2},{3,7},{7,3}} | collective-permute-start | bytes 9437192 | tf_op jit(solution)/shard_map/ppermute | solution.py:233
  1744.1 417.3 %collective-permute-start.7 = (f32[1024,1024]{1,0:T(8,128)}, f32[1024,1024]{1,0:T(8,128)}, u32[]{:S(2)}, u32[]{:S(2)}) collective-permute-start(f32[1024,1024]{1,0:T(8,128)} %reduce-scatter.23.cloned.1.call-done), channel_id=1, source_target_pairs={{0,4},{4,0},{1,5},{5,1},{2,6},{6,2},{3,7},{7,3}} | collective-permute-start | bytes 12582920 | tf_op jit(solution)/shard_map/ppermute | solution.py:233
  1745.6 168.0 %copy-start.11 = (f32[256,1024]{1,0:T(8,128)S(1)}, f32[256,1024]{1,0:T(8,128)}, u32[]{:S(2)}) copy-start(f32[256,1024]{1,0:T(8,128)} %reduce-scatter.15.cloned.1.call-done) | copy-start | bytes 3145732
  1745.6 169.4 %copy-start.12 = (f32[256,1024]{1,0:T(8,128)S(1)}, f32[256,1024]{1,0:T(8,128)}, u32[]{:S(2)}) copy-start(f32[256,1024]{1,0:T(8,128)} %reduce-scatter.13.cloned.1.call-done) | copy-start | bytes 3145732
  1795.2 117.8 %copy-start.13 = (f32[256,1024]{1,0:T(8,128)}, f32[256,1024]{1,0:T(8,128)S(1)}, u32[]{:S(2)}) copy-start(f32[256,1024]{1,0:T(8,128)S(1)} %collective-permute-done.3) | copy-start | bytes 3145732
  1865.2 299.4 %collective-permute-start.5 = (f32[256,4096]{1,0:T(8,128)}, f32[256,4096]{1,0:T(8,128)}, u32[]{:S(2)}, u32[]{:S(2)}) collective-permute-start(f32[256,4096]{1,0:T(8,128)} %reduce-scatter.19.cloned.1.call-done), channel_id=1, source_target_pairs={{0,4},{4,0},{1,5},{5,1},{2,6},{6,2},{3,7},{7,3}} | collective-permute-start | bytes 12582920 | tf_op jit(solution)/shard_map/ppermute | solution.py:233
  2031.7 136.0 %collective-permute-start.4 = (f32[256,4096]{1,0:T(8,128)}, f32[256,4096]{1,0:T(8,128)}, u32[]{:S(2)}, u32[]{:S(2)}) collective-permute-start(f32[256,4096]{1,0:T(8,128)} %reduce-scatter.17.cloned.1.call-done), channel_id=1, source_target_pairs={{0,4},{4,0},{1,5},{5,1},{2,6},{6,2},{3,7},{7,3}} | collective-permute-start | bytes 12582920 | tf_op jit(solution)/shard_map/ppermute | solution.py:233
  2152.9 92.1 %collective-permute-start.6 = (f32[1024,1024]{1,0:T(8,128)}, f32[1024,1024]{1,0:T(8,128)}, u32[]{:S(2)}, u32[]{:S(2)}) collective-permute-start(f32[1024,1024]{1,0:T(8,128)} %reduce-scatter.21.cloned.1.call-done), channel_id=1, source_target_pairs={{0,4},{4,0},{1,5},{5,1},{2,6},{6,2},{3,7},{7,3}} | collective-permute-start | bytes 12582920 | tf_op jit(solution)/shard_map/ppermute | solution.py:233
  2164.6 80.3 %copy-start.9 = (f32[1024,1024]{1,0:T(8,128)S(1)}, f32[1024,1024]{1,0:T(8,128)}, u32[]{:S(2)}) copy-start(f32[1024,1024]{1,0:T(8,128)} %reduce-scatter.21.cloned.1.call-done) | copy-start | bytes 12582916
  (53 other events, 893.5 us)
Sparse Core Ops, SparseCore 0:
  12.5 46.9 all-gather.18
  60.9 19.5 all-gather.20
  82.6 55.7 all-gather.22
  140.3 55.7 all-gather.24
  197.5 43.6 all-gather.26
  242.5 19.5 all-gather.28
  264.2 55.7 all-gather.30
  322.0 55.7 all-gather.32
  1270.9 38.2 reduce-scatter.14
  1360.4 38.2 reduce-scatter.12
  1401.2 90.5 reduce-scatter.10
  1532.2 90.5 reduce-scatter.8
  1625.3 118.7 reduce-scatter.22
  1746.5 118.7 reduce-scatter.18
  1868.7 42.2 all-reduce.1
  1913.4 118.2 reduce-scatter.16
  2034.1 118.7 reduce-scatter.20
